TPU v7x, 32 devices: a whole 2x2x4 slice. The times are simulated.
32 devices in a mesh: ctx: 8 (over z, core), tp: 4 (over y, x).
Axes of the slice: x: 2, y: 2, z: 4, core: 2. Of those that a mesh axis runs over, the one named last changes fastest.
Arguments:
- act_codes: bfloat16 [2048, 4096], P(('ctx', 'tp')), may hold values from -6 to 6
- scale_exps: int32 [2048, 32], P(('ctx', 'tp')), may hold values from -2 to 2
- weight: bfloat16 [4096, 6144], P(None, 'tp'), may hold values from -0.09375 to 0.09375
- grad_out: bfloat16 [2048, 6144], P('ctx', 'tp'), may hold values from -6 to 6
Outputs:
- grad_input: bfloat16 [2048, 4096], P(('ctx', 'tp'))
- grad_weight: float32 [4096, 6144], P('ctx', 'tp')
All inputs are finite; a program needn't handle non-finite values.
Results may differ from a plain program's by a relative error of at most 0.023.
Values may be sent and summed in bfloat16 or wider, within the bound.
No kernel may reach another device: no remote copies, remote signals or barrier semaphores. Data moves between devices by JAX's collectives and lax.ppermute only.
A program may use at most 64 MiB of HBM per device.

v0:
```python
import jax
import jax.numpy as jnp
from jax import lax
from jax.sharding import PartitionSpec as P


def dequantize(codes, exponents, block):
    tok_rows, width = codes.shape
    scales = jnp.exp2(exponents.astype(jnp.float32))
    blocked = (
        codes.astype(jnp.float32).reshape(tok_rows, width // block, block) * scales[:, :, None]
    )
    return blocked.reshape(tok_rows, width).astype(jnp.bfloat16)


def body(act_codes, scale_exps, weight, grad_out):
    width = act_codes.shape[1]
    block = width // scale_exps.shape[1]
    acts = dequantize(act_codes, scale_exps, block)
    add_acts = lax.all_gather(acts, "tp", axis=0, tiled=True)
    grads = grad_out
    partial_sum = lax.dot_general(
        add_acts, grads, (((0,), (0,)), ((), ())), preferred_element_type=jnp.float32
    )
    summed = lax.psum_scatter(
        partial_sum.astype(jnp.bfloat16), "ctx", scatter_dimension=0, tiled=True
    ).astype(jnp.float32)
    tokens_all = grad_out.shape[0] * lax.axis_size("ctx")
    grad_weight = summed * lax.rsqrt(jnp.float32(tokens_all))
    grads = grad_out
    grad_input = lax.psum_scatter(
        lax.dot_general(
            grads, weight, (((1,), (1,)), ((), ())), preferred_element_type=jnp.float32
        ).astype(jnp.bfloat16),
        "tp",
        scatter_dimension=0,
        tiled=True,
    )
    return (grad_input, grad_weight)


def solution(mesh):
    placed = (P(("ctx", "tp"), None), P(("ctx", "tp"), None), P(None, "tp"), P("ctx", "tp"))
    return jax.shard_map(
        body,
        mesh=mesh,
        in_specs=placed,
        out_specs=(P(("ctx", "tp"), None), P("ctx", "tp")),
        check_vma=False,
    )
```

profile of v0, /device:TPU:0, one launch (start us, length us, event | category | flops | bytes accessed | tf_op | source)
XLA Modules:
  0.0 230.3 jit_solution(15797501050247371986)
XLA Ops:
  7.2 0.0 copy-start
  7.2 0.0 all-gather.2.cloned.1.call-start
  7.2 0.8 multiply_exponential_fusion
  8.0 0.1 copy.6
  8.1 0.3 mul.17
  8.4 2.4 %fusion = bf16[64,4096]{1,0:T(8,128)(2,1)} fusion(f32[8,8,32,128]{3,2,1,0:T(8,128)S(1)} %bitcast.9, bf16[64,4096]{1,0:T(8,128)(2,1)} %param.4), kind=kLoop, calls=%fused_computation.4 | loop fusion | flops 786432 | bytes 2097152 | tf_op jit(solution)/shard_map/convert_element_type | solution.py:13
  10.9 0.0 all-gather.2.cloned.1.call-update
  10.9 0.0 reduce-scatter.5.cloned.1.call-start
  10.9 38.0 %all-gather.2.cloned.1.call-done = bf16[256,4096]{1,0:T(8,128)(2,1)} async-done(((bf16[64,4096]{1,0:T(8,128)(2,1)}), bf16[256,4096]{1,0:T(8,128)(2,1)}) %all-gather.2.cloned.1.call-update) | async-done | bytes 2097168 | tf_op jit(solution)/shard_map/all_gather | solution.py:20
  49.0 0.0 copy-done
  49.0 8.3 %convolution_convert_fusion = bf16[4096,1536]{1,0:T(8,128)(2,1)} fusion(bf16[256,4096]{1,0:T(8,128)(2,1)} %all-gather.2.cloned.1.call-done, bf16[256,1536]{1,0:T(8,128)(2,1)S(1)} %copy-done), kind=kOutput, calls=%fused_computation | convolution fusion | flops 3227516928 | bytes 15466496 | tf_op jit(solution)/shard_map/dot_general | solution.py:22
  57.2 0.0 reduce-scatter.5.cloned.1.call-update
  57.3 0.0 reduce-scatter.3.cloned.1.call-start
  57.3 13.9 %convolution_convert_fusion.1 = bf16[256,4096]{1,0:T(8,128)(2,1)} fusion(bf16[256,1536]{1,0:T(8,128)(2,1)S(1)} %copy-done, bf16[4096,1536]{1,0:T(8,128)(2,1)} %param.6), kind=kOutput, calls=%fused_computation.1 | convolution fusion | flops 3222274048 | bytes 15466496 | tf_op jit(solution)/shard_map/dot_general | solution.py:32
  71.2 0.0 reduce-scatter.3.cloned.1.call-update
  71.2 115.3 %reduce-scatter.5.cloned.1.call-done = bf16[512,1536]{1,0:T(8,128)(2,1)} async-done(((bf16[4096,1536]{1,0:T(8,128)(2,1)}), bf16[512,1536]{1,0:T(8,128)(2,1)}) %reduce-scatter.5.cloned.1.call-update) | async-done | bytes 1572880 | tf_op jit(solution)/shard_map/reduce_scatter | solution.py:25
  186.6 3.5 %convert_multiply_fusion = f32[512,1536]{1,0:T(8,128)} fusion(bf16[512,1536]{1,0:T(8,128)(2,1)} %reduce-scatter.5.cloned.1.call-done), kind=kLoop, calls=%fused_computation.2 | loop fusion | flops 1572864 | bytes 4718592 | tf_op jit(solution)/shard_map/mul | solution.py:29
  190.1 33.7 %reduce-scatter.3.cloned.1.call-done = bf16[64,4096]{1,0:T(8,128)(2,1)} async-done(((bf16[256,4096]{1,0:T(8,128)(2,1)}), bf16[64,4096]{1,0:T(8,128)(2,1)}) %reduce-scatter.3.cloned.1.call-update) | async-done | bytes 524304 | tf_op jit(solution)/shard_map/reduce_scatter | solution.py:31
Async XLA Ops:
  7.2 41.8 %copy-start = (bf16[256,1536]{1,0:T(8,128)(2,1)S(1)}, bf16[256,1536]{1,0:T(8,128)(2,1)}, u32[]{:S(2)}) copy-start(bf16[256,1536]{1,0:T(8,128)(2,1)} %param.7) | copy-start | bytes 2359300
  7.2 41.8 %all-gather.2.cloned.1.call-start = ((), (), s32[]{:S(2)}) async-start(), calls=%async_computation.3 | async-start | bytes 2621440 | tf_op jit(solution)/shard_map/all_gather | solution.py:20
  10.9 175.7 %reduce-scatter.5.cloned.1.call-start = ((), (), s32[]{:S(2)}) async-start(), calls=%async_computation.4 | async-start | bytes 14155776 | tf_op jit(solution)/shard_map/reduce_scatter | solution.py:25
  57.3 166.5 %reduce-scatter.3.cloned.1.call-start = ((), (), s32[]{:S(2)}) async-start(), calls=%async_computation.2 | async-start | bytes 2621440 | tf_op jit(solution)/shard_map/reduce_scatter | solution.py:31
Sparse Core Ops, SparseCore 0:
  11.0 37.8 all-gather.1
  57.4 129.1 reduce-scatter.4
  190.1 33.6 reduce-scatter.2
where the time goes:
time: 231 us; the launch traced here: 230 us
  waiting for transfers between devices  187 us (81%)
  matrix products  22.2 us (10%)
  between operations  13.8 us (6%)
  other arithmetic  6.73 us (3%)
    reduce_scatter x1, waiting for transfers between devices, body(): lax.psum_scatter(partial_sum.astype(jnp.bfloat16), 'ctx', scatter_dimensi...  115 us
    all_gather x1, waiting for transfers between devices, body(): add_acts = lax.all_gather(acts, 'tp', axis=0, tiled=True)  38 us
    reduce_scatter x1, waiting for transfers between devices, body(): lax.psum_scatter(lax.dot_general(grads, weight, (((1,), (1,)), ((), ())),...  33.7 us
    dot_general x1, matrix products, body(): lax.dot_general(grads, weight, (((1,), (1,)), ((), ())), preferred_elemen...  13.9 us
    dot_general x1, matrix products, body(): lax.dot_general(add_acts, grads, (((0,), (0,)), ((), ())), preferred_elem...  8.29 us
  transfers between devices with their start and end apart: 3, of which 3 were waited for; matrix products, arithmetic and copies ran while one was open for 8% of the time, Pallas kernels for 0%

commit v1 on v0

v1 whole, which is shorter than its diff:
```python
import functools

import jax
import jax.numpy as jnp
from jax import lax
from jax.experimental import pallas as pl
from jax.experimental.pallas import tpu as pltpu
from jax.sharding import PartitionSpec as P

VMEM = pl.BlockSpec(memory_space=pltpu.VMEM)


def ring_order(length):
    return list(range(0, length, 2)) + list(range(length - 1 - (length % 2), 0, -2))


def prepare_kernel(order, block, codes_ref, exps_ref, *out_refs):
    chips = len(order)
    wide = out_refs[0].shape[-1]
    per = wide // block
    chip = lax.axis_index("ctx") // 2
    exps = exps_ref[...].astype(jnp.float32).T
    for step, out_ref in enumerate(out_refs):
        dest = jnp.int32(0)
        for i in range(chips):
            dest = dest + jnp.where(chip == order[i], order[(i + step) % chips], 0)
        chosen = jnp.zeros((exps.shape[0], per), jnp.float32)
        for k in range(chips):
            chosen = jnp.where(dest == k, exps[:, per * k : per * (k + 1)], chosen)
        scales = jnp.exp2(chosen)
        for j in range(per):
            column = pl.multiple_of(dest * wide + j * block, block)
            codes = codes_ref[:, pl.ds(column, block)].astype(jnp.float32)
            out_ref[:, j * block : (j + 1) * block] = (codes * scales[:, j : j + 1]).astype(
                jnp.bfloat16
            )


def prepare(codes, exponents, order):
    rows, width = codes.shape
    chips = len(order)
    out = jax.ShapeDtypeStruct((rows, width // chips), jnp.bfloat16)
    return pl.pallas_call(
        functools.partial(prepare_kernel, order, width // exponents.shape[1]),
        out_shape=[out] * chips,
        in_specs=[VMEM] * 2,
        out_specs=[VMEM] * chips,
        cost_estimate=pl.CostEstimate(
            flops=2 * rows * width, bytes_accessed=4 * rows * width, transcendentals=0
        ),
    )(codes, exponents.T)


def tdot(a, b):
    return lax.dot_general(a, b, (((0,), (0,)), ((), ())), preferred_element_type=jnp.float32)


def added(terms):
    return sum(t.astype(jnp.float32) for t in terms).astype(jnp.bfloat16)


def body(act_codes, scale_exps, weight, grad_out):
    width = act_codes.shape[1]
    n_ctx, n_tp = lax.axis_size("ctx"), lax.axis_size("tp")
    chips = n_ctx // 2
    tp = lax.axis_index("tp")
    rows = act_codes.shape[0]
    tokens = grad_out.shape[0]
    out_rows = width // n_ctx
    core = lax.axis_index("ctx") % 2
    order = ring_order(chips)
    half = tokens // 2

    swap = [(i, i ^ 1) for i in range(n_ctx)]

    def shift(step):
        return [
            (2 * order[i] + c, 2 * order[(i + step) % chips] + c)
            for i in range(chips)
            for c in range(2)
        ]

    def peers(j):
        return [(i, i ^ j) for i in range(n_tp)]

    every = jnp.zeros((chips * tokens, grad_out.shape[1]), jnp.bfloat16)
    every = lax.dynamic_update_slice(every, grad_out, (0, 0))
    moving = lax.ppermute(grad_out, "ctx", shift(1))
    every = lax.dynamic_update_slice(every, moving, (tokens, 0))
    moving = [moving[:half], moving[half:]]
    for step in range(2, chips):
        for h in range(2):
            moving[h] = lax.ppermute(moving[h], "ctx", shift(1))
            if step < chips - 1 or h == 0:
                every = lax.dynamic_update_slice(every, moving[h], (step * tokens + h * half, 0))

    pieces = list(prepare(act_codes, scale_exps, order))
    for step in range(1, chips):
        pieces[step] = lax.ppermute(pieces[step], "ctx", shift(step))
    pieces = jnp.stack(pieces)
    got = {0: pieces}
    if n_tp == 4:
        for j in (1, 2):
            got[j] = lax.ppermute(pieces, "tp", peers(j))
        middle = chips // 2
        first = lax.ppermute(got[1][:middle], "tp", peers(2))
        second = lax.ppermute(got[2][middle:], "tp", peers(1))
    else:
        for j in range(1, n_tp):
            got[j] = lax.ppermute(pieces, "tp", peers(j))
    if n_tp == 4:
        got[3] = None
    sides = []
    for side in range(2):
        acts = jnp.zeros((chips, n_tp, rows, out_rows), jnp.bfloat16)
        for j, part in got.items():
            blocks = [(0, part)] if part is not None else [(0, first), (middle, second)]
            for at, block in blocks:
                block = jnp.where(core == side, block[..., :out_rows], block[..., out_rows:])
                acts = lax.dynamic_update_slice(acts, block[:, None], (at, tp ^ j, 0, 0))
        sides.append(acts.reshape(chips * tokens, out_rows))

    outs = []
    span = width // 2
    bits = [1 << b for b in range(n_tp.bit_length() - 1)]
    for h in range(2):
        part = lax.dot_general(
            grad_out,
            lax.slice_in_dim(weight, h * span, (h + 1) * span),
            (((1,), (1,)), ((), ())),
            preferred_element_type=jnp.float32,
        ).astype(jnp.bfloat16)
        held = {j: [lax.dynamic_slice_in_dim(part, (tp ^ j) * rows, rows, 0)] for j in range(n_tp)}
        for bit in bits if h == 0 else bits[::-1]:
            leaving = [j for j in held if j & bit]
            sent = jnp.stack([added(held.pop(j)) for j in leaving])
            sent = lax.ppermute(sent, "tp", peers(bit))
            for i, j in enumerate(leaving):
                held[j ^ bit].append(sent[i])
        outs.append(added(held[0]))
    grad_input = jnp.concatenate(outs, axis=1)

    scale = lax.rsqrt(jnp.float32(tokens * n_ctx))
    own, other = sides
    most = chips * tokens - half
    last = moving[1]
    handed = tdot(other[:most], every[:most])
    kept = tdot(own[:most], every[:most])
    handed, kept = lax.optimization_barrier((handed, kept))
    handed = (handed + tdot(other[most:], last)).astype(jnp.bfloat16)
    handed = lax.ppermute(handed, "ctx", swap)
    kept = lax.optimization_barrier(kept + tdot(own[most:], last))
    grad_weight = (kept + handed.astype(jnp.float32)) * scale
    return (grad_input, grad_weight)


def solution(mesh):
    placed = (P(("ctx", "tp"), None), P(("ctx", "tp"), None), P(None, "tp"), P("ctx", "tp"))

    return jax.shard_map(
        body,
        mesh=mesh,
        in_specs=placed,
        out_specs=(P(("ctx", "tp"), None), P("ctx", "tp")),
        check_vma=False,
    )
```

time: 231 us -> 98.7 us (0.43)
  waiting for transfers between devices: 187 us -> 46.5 us
  starting transfers between devices: 0.12 us -> 21 us
  between operations: 13.8 us -> 0.94 us
  matrix products: 22.2 us -> 15.4 us
  local copies, waits for them, and re-layouts: 0.43 us -> 4.01 us
  Pallas kernels: 0 us -> 2.86 us
    reduce_scatter x2 -> x0, waiting for transfers between devices: 149 us -> none  [the longest x1 115 us: body(): lax.psum_scatter(partial_sum.astype(jnp.bfloat16), 'ctx', scatter_dimensi...]
    ppermute x0 -> x17, waiting for transfers between devices: none -> 46.5 us  [the longest x4 21.1 us: body(): moving[h] = lax.ppermute(moving[h], 'ctx', shift(1))]
    all_gather x1 -> x0, waiting for transfers between devices: 38 us -> none  [body(): add_acts = lax.all_gather(acts, 'tp', axis=0, tiled=True)]
    ppermute x0 -> x17, starting transfers between devices: none -> 21 us  [the longest x3 6.2 us: body(): pieces[step] = lax.ppermute(pieces[step], 'ctx', shift(step))]
    dot_general x2 -> x6, matrix products: 22.2 us -> 15.4 us  [the longest x2 10.6 us: body(): lax.dot_general(grad_out, lax.slice_in_dim(weight, h * span, (h + 1) * sp...]
    another operation x0 -> x5, other arithmetic: none -> 3.07 us  [the longest x4 2.1 us: body(): sent = jnp.stack([added(held.pop(j)) for j in leaving])]
    pallas_call x0 -> x1, Pallas kernels: none -> 2.86 us  [prepare(): pl.pallas_call(functools.partial(prepare_kernel, order, width // exponent...]
  transfers between devices with their start and end apart: 3 -> 17, of which waited for: 3 -> 8; matrix products, arithmetic and copies ran while one was open for 8% -> 25% of each run, Pallas kernels for 0% -> 0%
where the time goes in v1:
time: 98.7 us; the launch traced here: 98.4 us
  waiting for transfers between devices  46.5 us (47%)
  starting transfers between devices  21 us (21%)
  matrix products  15.4 us (16%)
  other arithmetic  7.66 us (8%)
  local copies, waits for them, and re-layouts  4.01 us (4%)
  Pallas kernels  2.86 us (3%)
    ppermute x4, waiting for transfers between devices, body(): moving[h] = lax.ppermute(moving[h], 'ctx', shift(1))  21.1 us
    dot_general x2, matrix products, body(): lax.dot_general(grad_out, lax.slice_in_dim(weight, h * span, (h + 1) * sp...  10.6 us
    ppermute x3, waiting for transfers between devices, body(): pieces[step] = lax.ppermute(pieces[step], 'ctx', shift(step))  9.78 us
    ppermute x2, waiting for transfers between devices, body(): got[j] = lax.ppermute(pieces, 'tp', peers(j))  9.13 us
    ppermute x3, starting transfers between devices, body(): pieces[step] = lax.ppermute(pieces[step], 'ctx', shift(step))  6.2 us
    ppermute x1, waiting for transfers between devices, body(): first = lax.ppermute(got[1][:middle], 'tp', peers(2))  5.65 us
    dot_general x4, matrix products, tdot(): lax.dot_general(a, b, (((0,), (0,)), ((), ())), preferred_element_type=jn...  4.82 us
    ppermute x4, starting transfers between devices, body(): sent = lax.ppermute(sent, 'tp', peers(bit))  4.25 us
  transfers between devices with their start and end apart: 17, of which 8 were waited for; matrix products, arithmetic and copies ran while one was open for 25% of the time, Pallas kernels for 0%

profile of v1, /device:TPU:0, one launch (start us, length us, event | category | flops | bytes accessed | tf_op | source)
XLA Modules:
  0.0 98.4 jit_solution(9373925133542410783)
XLA Ops:
  0.6 2.9 %shard_map.59 = (bf16[64,1024]{1,0:T(8,128)(2,1)}, bf16[64,1024]{1,0:T(8,128)(2,1)}, bf16[64,1024]{1,0:T(8,128)(2,1)}, bf16[64,1024]{1,0:T(8,128)(2,1)}) custom-call(bf16[64,4096]{1,0:T(8,128)(2,1)} %codes_ref.1, s32[32,64]{1,0:T(8,128)} %bitcast.96), custom_call_target="tpu_custom_call" | custom-call | flops 524288 | bytes 1048576 | tf_op jit(solution)/shard_map/pallas_call | solution.py:43
  3.5 4.1 %collective-permute-start.4 = (bf16[64,1024]{1,0:T(8,128)(2,1)}, bf16[64,1024]{1,0:T(8,128)(2,1)S(1)}, u32[]{:S(2)}, u32[]{:S(2)}) collective-permute-start(bf16[64,1024]{1,0:T(8,128)(2,1)} %get-tuple-element.9), channel_id=1, source_target_pairs={{0,16},{4,20},{16,24},{20,28},{24,8},{28,12},{8,0},{12,4},{1,17},{... | collective-permute-start | bytes 393224 | tf_op jit(solution)/shard_map/ppermute | solution.py:99
  7.6 1.3 %collective-permute-start.5 = (bf16[64,1024]{1,0:T(8,128)(2,1)}, bf16[64,1024]{1,0:T(8,128)(2,1)S(1)}, u32[]{:S(2)}, u32[]{:S(2)}) collective-permute-start(bf16[64,1024]{1,0:T(8,128)(2,1)} %get-tuple-element.10), channel_id=1, source_target_pairs={{0,24},{4,28},{16,8},{20,12},{24,0},{28,4},{8,16},{12,20},{1,25},{... | collective-permute-start | bytes 393224 | tf_op jit(solution)/shard_map/ppermute | solution.py:99
  8.9 0.8 collective-permute-start.6
  9.7 2.1 %collective-permute-start.11 = (bf16[256,1536]{1,0:T(8,128)(2,1)}, bf16[256,1536]{1,0:T(8,128)(2,1)}, u32[]{:S(2)}, u32[]{:S(2)}) collective-permute-start(bf16[256,1536]{1,0:T(8,128)(2,1)} %param.7), channel_id=1, source_target_pairs={{0,16},{4,20},{16,24},{20,28},{24,8},{28,12},{8,0},{12,4},{1,17},{... | collective-permute-start | bytes 2359304 | tf_op jit(solution)/shard_map/ppermute | solution.py:88
  11.8 4.9 %fusion.5 = bf16[256,2048]{1,0:T(8,128)(2,1)S(1)} fusion(bf16[256,1536]{1,0:T(8,128)(2,1)} %param.7, bf16[4096,1536]{1,0:T(8,128)(2,1)} %param.6), kind=kOutput, calls=%fused_computation.8 | convolution fusion | flops 1611137024 | bytes 8126464 | tf_op jit(solution)/shard_map/dot_general | solution.py:127
  16.8 1.0 pad_maximum_fusion
  17.8 1.5 %collective-permute-start = (bf16[2,64,2048]{2,1,0:T(8,128)(2,1)}, bf16[2,64,2048]{2,1,0:T(8,128)(2,1)}, u32[]{:S(2)}, u32[]{:S(2)}) collective-permute-start(bf16[2,64,2048]{2,1,0:T(8,128)(2,1)} %pad_maximum_fusion), channel_id=1, source_target_pairs={{0,1},{1,0},{2,3},{3,2},{4,5},{5,4},{6,7},{7,6},{8,9},{9,8},{10,11... | collective-permute-start | bytes 1572872 | tf_op jit(solution)/shard_map/ppermute | solution.py:137
  19.3 0.0 copy-done
  19.3 5.6 %fusion.8 = bf16[256,2048]{1,0:T(8,128)(2,1)} fusion(bf16[256,1536]{1,0:T(8,128)(2,1)S(1)} %copy-done.3, bf16[4096,1536]{1,0:T(8,128)(2,1)} %param.6), kind=kOutput, calls=%fused_computation.9 | convolution fusion | flops 1611137024 | bytes 8126464 | tf_op jit(solution)/shard_map/dot_general | solution.py:127
  24.9 0.2 dynamic_update_slice.50
  25.2 1.1 %dynamic-slice_bitcast_fusion.1 = (bf16[1,64,2048]{2,1,0:T(8,128)(2,1)S(1)}, bf16[1,64,2048]{2,1,0:T(8,128)(2,1)S(1)}) fusion(bf16[256,2048]{1,0:T(8,128)(2,1)} %fusion.8, s32[]{:T(128)S(6)} %select_n.96, s32[]{:T(128)S(6)} %select_n.95), kind=kLoop, calls=%fused_computation.43 | loop fusion | bytes 1048584 | tf_op jit(solution)/shard_map/stack | solution.py:136
  26.3 0.0 copy-start.1
  26.3 0.0 copy-start.2
  26.3 0.1 pad_maximum_fusion.1
  26.3 0.0 collective-permute-done.4
  26.3 1.6 %collective-permute-start.2 = (bf16[2,64,2048]{2,1,0:T(8,128)(2,1)S(1)}, bf16[2,64,2048]{2,1,0:T(8,128)(2,1)S(1)}, u32[]{:S(2)}, u32[]{:S(2)}) collective-permute-start(bf16[2,64,2048]{2,1,0:T(8,128)(2,1)S(1)} %pad_maximum_fusion.1), channel_id=1, source_target_pairs={{0,2},{1,3},{2,0},{3,1},{4,6},{5,7},{6,4},{7,5},{8,10},{9,11},{10,... | collective-permute-start | bytes 1572872 | tf_op jit(solution)/shard_map/ppermute | solution.py:137
  27.9 0.0 collective-permute-done.5
  27.9 9.8 %collective-permute-done.6 = bf16[64,1024]{1,0:T(8,128)(2,1)} collective-permute-done((bf16[64,1024]{1,0:T(8,128)(2,1)}, bf16[64,1024]{1,0:T(8,128)(2,1)}, u32[]{:S(2)}, u32[]{:S(2)}) %collective-permute-start.6) | collective-permute-done | bytes 131104 | tf_op jit(solution)/shard_map/ppermute | solution.py:99
  37.7 1.0 pad_maximum_fusion.3
  38.7 1.6 %collective-permute-start.7 = (bf16[4,64,1024]{2,1,0:T(8,128)(2,1)S(1)}, bf16[4,64,1024]{2,1,0:T(8,128)(2,1)S(1)}, u32[]{:S(2)}, u32[]{:S(2)}) collective-permute-start(bf16[4,64,1024]{2,1,0:T(8,128)(2,1)S(1)} %pad_maximum_fusion.3), channel_id=1, source_target_pairs={{0,1},{1,0},{2,3},{3,2},{4,5},{5,4},{6,7},{7,6},{8,9},{9,8},{10,11... | collective-permute-start | bytes 1572872 | tf_op jit(solution)/shard_map/ppermute | solution.py:104
  40.2 1.5 %collective-permute-start.8 = (bf16[4,64,1024]{2,1,0:T(8,128)(2,1)S(1)}, bf16[4,64,1024]{2,1,0:T(8,128)(2,1)S(1)}, u32[]{:S(2)}, u32[]{:S(2)}) collective-permute-start(bf16[4,64,1024]{2,1,0:T(8,128)(2,1)S(1)} %pad_maximum_fusion.3), channel_id=1, source_target_pairs={{0,2},{1,3},{2,0},{3,1},{4,6},{5,7},{6,4},{7,5},{8,10},{9,11},{10,... | collective-permute-start | bytes 1572872 | tf_op jit(solution)/shard_map/ppermute | solution.py:104
  41.8 0.1 broadcast.6.clone
  41.9 0.1 bitcast_dynamic-update-slice_fusion.2
  41.9 0.1 broadcast.6.clone.1
  42.0 0.1 bitcast_dynamic-update-slice_fusion.5
  42.1 0.0 collective-permute-done
  42.1 1.0 %fusion.21 = bf16[1,64,2048]{2,1,0:T(8,128)(2,1)S(1)} fusion(bf16[2,64,2048]{2,1,0:T(8,128)(2,1)} %collective-permute-done, bf16[256,2048]{1,0:T(8,128)(2,1)S(1)} %copy-done.1, s32[]{:T(128)S(6)} %select_n.96), kind=kLoop, calls=%fused_computation.30 | loop fusion | flops 524288 | bytes 786436 | tf_op jit(solution)/shard_map/stack | solution.py:136
  43.2 0.6 collective-permute-start.1
  43.7 0.0 collective-permute-done.2
  43.7 0.1 fusion.22
  43.8 0.6 collective-permute-start.3
  44.4 9.1 %collective-permute-done.7 = bf16[4,64,1024]{2,1,0:T(8,128)(2,1)S(1)} collective-permute-done((bf16[4,64,1024]{2,1,0:T(8,128)(2,1)S(1)}, bf16[4,64,1024]{2,1,0:T(8,128)(2,1)S(1)}, u32[]{:S(2)}, u32[]{:S(2)}) %collective-permute-start.7) | collective-permute-done | bytes 524320 | tf_op jit(solution)/shard_map/ppermute | solution.py:104
  53.6 1.6 %collective-permute-start.9 = (bf16[2,64,1024]{2,1,0:T(8,128)(2,1)S(1)}, bf16[2,64,1024]{2,1,0:T(8,128)(2,1)S(1)}, u32[]{:S(2)}, u32[]{:S(2)}) collective-permute-start(bf16[2,64,1024]{2,1,0:T(8,128)(2,1)S(1)} %slice.121), channel_id=1, source_target_pairs={{0,2},{1,3},{2,0},{3,1},{4,6},{5,7},{6,4},{7,5},{8,10},{9,11},{10,... | collective-permute-start | bytes 786440 | tf_op jit(solution)/shard_map/ppermute | solution.py:106
  55.2 0.0 collective-permute-done.8
  55.2 1.6 %collective-permute-start.10 = (bf16[2,64,1024]{2,1,0:T(8,128)(2,1)S(1)}, bf16[2,64,1024]{2,1,0:T(8,128)(2,1)S(1)}, u32[]{:S(2)}, u32[]{:S(2)}) collective-permute-start(bf16[2,64,1024]{2,1,0:T(8,128)(2,1)S(1)} %slice.124), channel_id=1, source_target_pairs={{0,1},{1,0},{2,3},{3,2},{4,5},{5,4},{6,7},{7,6},{8,9},{9,8},{10,11... | collective-permute-start | bytes 786440 | tf_op jit(solution)/shard_map/ppermute | solution.py:107
  56.7 0.1 bitcast_dynamic-update-slice_fusion.1
  56.8 0.1 bitcast_dynamic-update-slice_fusion
  57.0 0.0 collective-permute-done.11
  57.0 1.2 %fusion.25 = (bf16[128,1536]{1,0:T(8,128)(2,1)S(1)}, bf16[128,1536]{1,0:T(8,128)(2,1)S(1)}) fusion(bf16[256,1536]{1,0:T(8,128)(2,1)} %collective-permute-done.11), kind=kLoop, calls=%fused_computation.56 | loop fusion | bytes 1572864 | tf_op jit(solution)/shard_map/slice | solution.py:90
  58.1 0.1 collective-permute-start.12
  58.2 1.2 %constant_dynamic-update-slice_fusion.3 = bf16[1024,1536]{1,0:T(8,128)(2,1)S(1)} fusion(bf16[1024,1536]{1,0:T(8,128)(2,1)S(1)} %dynamic_update_slice.50, bf16[256,1536]{1,0:T(8,128)(2,1)} %collective-permute-done.11), kind=kLoop, calls=%fused_computation.55 | loop fusion | bytes 1572864 | tf_op jit(solution)/shard_map/dynamic_update_slice | solution.py:89
  59.4 5.7 %collective-permute-done.9 = bf16[2,64,1024]{2,1,0:T(8,128)(2,1)S(1)} collective-permute-done((bf16[2,64,1024]{2,1,0:T(8,128)(2,1)S(1)}, bf16[2,64,1024]{2,1,0:T(8,128)(2,1)S(1)}, u32[]{:S(2)}, u32[]{:S(2)}) %collective-permute-start.9) | collective-permute-done | bytes 262176 | tf_op jit(solution)/shard_map/ppermute | solution.py:106
  65.0 0.0 collective-permute-start.13
  65.1 0.0 collective-permute-done.10
  65.1 0.1 bitcast_dynamic-update-slice_fusion.6
  65.2 2.0 %collective-permute-done.12 = bf16[128,1536]{1,0:T(8,128)(2,1)S(1)} collective-permute-done((bf16[128,1536]{1,0:T(8,128)(2,1)S(1)}, bf16[128,1536]{1,0:T(8,128)(2,1)S(1)}, u32[]{:S(2)}, u32[]{:S(2)}) %collective-permute-start.12) | collective-permute-done | bytes 393248 | tf_op jit(solution)/shard_map/ppermute | solution.py:93
  67.2 1.2 %collective-permute-start.14 = (bf16[128,1536]{1,0:T(8,128)(2,1)S(1)}, bf16[128,1536]{1,0:T(8,128)(2,1)S(1)}, u32[]{:S(2)}, u32[]{:S(2)}) collective-permute-start(bf16[128,1536]{1,0:T(8,128)(2,1)S(1)} %collective-permute-done.12), channel_id=1, source_target_pairs={{0,16},{4,20},{16,24},{20,28},{24,8},{28,12},{8,0},{12,4},{1,17},{... | collective-permute-start | bytes 1179656 | tf_op jit(solution)/shard_map/ppermute | solution.py:93
  68.4 8.6 %collective-permute-done.13 = bf16[128,1536]{1,0:T(8,128)(2,1)S(1)} collective-permute-done((bf16[128,1536]{1,0:T(8,128)(2,1)S(1)}, bf16[128,1536]{1,0:T(8,128)(2,1)S(1)}, u32[]{:S(2)}, u32[]{:S(2)}) %collective-permute-start.13) | collective-permute-done | bytes 393248 | tf_op jit(solution)/shard_map/ppermute | solution.py:93
  77.0 0.9 collective-permute-start.15
  78.0 7.5 %collective-permute-done.14 = bf16[128,1536]{1,0:T(8,128)(2,1)S(1)} collective-permute-done((bf16[128,1536]{1,0:T(8,128)(2,1)S(1)}, bf16[128,1536]{1,0:T(8,128)(2,1)S(1)}, u32[]{:S(2)}, u32[]{:S(2)}) %collective-permute-start.14) | collective-permute-done | bytes 393248 | tf_op jit(solution)/shard_map/ppermute | solution.py:93
  85.5 1.8 %fusion.11 = f32[512,1536]{1,0:T(8,128)S(1)} fusion(bf16[1024,1536]{1,0:T(8,128)(2,1)S(1)} %constant_dynamic-update-slice_fusion, bf16[1024,512]{1,0:T(8,128)(2,1)S(1)} %bitcast.91), kind=kOutput, calls=%fused_computation.10 | convolution fusion | flops 1409286144 | bytes 6815744 | tf_op jit(solution)/shard_map/dot_general | solution.py:55
  87.3 1.8 %fusion.13 = f32[512,1536]{1,0:T(8,128)S(1)} fusion(bf16[1024,1536]{1,0:T(8,128)(2,1)S(1)} %constant_dynamic-update-slice_fusion, bf16[1024,512]{1,0:T(8,128)(2,1)S(1)} %bitcast.89), kind=kOutput, calls=%fused_computation.12 | convolution fusion | flops 1409286144 | bytes 6815744 | tf_op jit(solution)/shard_map/dot_general | solution.py:55
  89.1 3.0 %collective-permute-done.15 = bf16[128,1536]{1,0:T(8,128)(2,1)S(1)} collective-permute-done((bf16[128,1536]{1,0:T(8,128)(2,1)S(1)}, bf16[128,1536]{1,0:T(8,128)(2,1)S(1)}, u32[]{:S(2)}, u32[]{:S(2)}) %collective-permute-start.15) | collective-permute-done | bytes 393248 | tf_op jit(solution)/shard_map/ppermute | solution.py:93
  92.1 0.6 fusion.4
  92.7 0.1 collective-permute-start.16
  92.8 0.0 collective-permute-done.1
  92.8 1.1 %fusion.19 = bf16[64,2048]{1,0:T(8,128)(2,1)S(1)} fusion(bf16[2,64,2048]{2,1,0:T(8,128)(2,1)} %collective-permute-done, bf16[1,64,2048]{2,1,0:T(8,128)(2,1)S(1)} %collective-permute-done.1, bf16[256,2048]{1,0:T(8,128)(2,1)S(1)} %copy-done.1, s32[]{:T(128)S(6)} %select_n.93), kind=kLoop, calls=%fused_computation.26 | loop fusion | flops 786432 | bytes 1048580 | tf_op jit(solution)/shard_map/convert_element_type | solution.py:59
  93.9 0.0 collective-permute-done.3
  93.9 0.1 fusion.17
  94.0 0.8 pad_maximum_fusion.2
  94.8 0.6 convolution_add_fusion.1
  95.4 0.8 collective-permute-done.16
  96.2 2.1 %add_multiply_fusion = f32[512,1536]{1,0:T(8,128)} fusion(f32[512,1536]{1,0:T(8,128)S(1)} %convolution_add_fusion.1, bf16[512,1536]{1,0:T(8,128)(2,1)S(1)} %collective-permute-done.16), kind=kLoop, calls=%fused_computation.6 | loop fusion | flops 2359296 | bytes 7864320 | tf_op jit(solution)/shard_map/mul | solution.py:153
  (16 shorter events, 0.2 us)
Async XLA Ops:
  3.5 22.8 %collective-permute-start.4 = (bf16[64,1024]{1,0:T(8,128)(2,1)}, bf16[64,1024]{1,0:T(8,128)(2,1)S(1)}, u32[]{:S(2)}, u32[]{:S(2)}) collective-permute-start(bf16[64,1024]{1,0:T(8,128)(2,1)} %get-tuple-element.9), channel_id=1, source_target_pairs={{0,16},{4,20},{16,24},{20,28},{24,8},{28,12},{8,0},{12,4},{1,17},{... | collective-permute-start | bytes 393224 | tf_op jit(solution)/shard_map/ppermute | solution.py:99
  7.6 20.4 %collective-permute-start.5 = (bf16[64,1024]{1,0:T(8,128)(2,1)}, bf16[64,1024]{1,0:T(8,128)(2,1)S(1)}, u32[]{:S(2)}, u32[]{:S(2)}) collective-permute-start(bf16[64,1024]{1,0:T(8,128)(2,1)} %get-tuple-element.10), channel_id=1, source_target_pairs={{0,24},{4,28},{16,8},{20,12},{24,0},{28,4},{8,16},{12,20},{1,25},{... | collective-permute-start | bytes 393224 | tf_op jit(solution)/shard_map/ppermute | solution.py:99
  8.9 28.8 %collective-permute-start.6 = (bf16[64,1024]{1,0:T(8,128)(2,1)}, bf16[64,1024]{1,0:T(8,128)(2,1)}, u32[]{:S(2)}, u32[]{:S(2)}) collective-permute-start(bf16[64,1024]{1,0:T(8,128)(2,1)} %get-tuple-element.11), channel_id=1, source_target_pairs={{0,8},{4,12},{16,0},{20,4},{24,16},{28,20},{8,24},{12,28},{1,9},{5... | collective-permute-start | bytes 393224 | tf_op jit(solution)/shard_map/ppermute | solution.py:99
  9.7 47.3 %collective-permute-start.11 = (bf16[256,1536]{1,0:T(8,128)(2,1)}, bf16[256,1536]{1,0:T(8,128)(2,1)}, u32[]{:S(2)}, u32[]{:S(2)}) collective-permute-start(bf16[256,1536]{1,0:T(8,128)(2,1)} %param.7), channel_id=1, source_target_pairs={{0,16},{4,20},{16,24},{20,28},{24,8},{28,12},{8,0},{12,4},{1,17},{... | collective-permute-start | bytes 2359304 | tf_op jit(solution)/shard_map/ppermute | solution.py:88
  11.8 7.5 %copy-start.3 = (bf16[256,1536]{1,0:T(8,128)(2,1)S(1)}, bf16[256,1536]{1,0:T(8,128)(2,1)}, u32[]{:S(2)}) copy-start(bf16[256,1536]{1,0:T(8,128)(2,1)} %param.7) | copy-start | bytes 2359300
  16.8 2.5 %copy-start = (bf16[256,2048]{1,0:T(8,128)(2,1)}, bf16[256,2048]{1,0:T(8,128)(2,1)S(1)}, u32[]{:S(2)}) copy-start(bf16[256,2048]{1,0:T(8,128)(2,1)S(1)} %fusion.5) | copy-start | bytes 3145732
  17.8 24.3 %collective-permute-start = (bf16[2,64,2048]{2,1,0:T(8,128)(2,1)}, bf16[2,64,2048]{2,1,0:T(8,128)(2,1)}, u32[]{:S(2)}, u32[]{:S(2)}) collective-permute-start(bf16[2,64,2048]{2,1,0:T(8,128)(2,1)} %pad_maximum_fusion), channel_id=1, source_target_pairs={{0,1},{1,0},{2,3},{3,2},{4,5},{5,4},{6,7},{7,6},{8,9},{9,8},{10,11... | collective-permute-start | bytes 1572872 | tf_op jit(solution)/shard_map/ppermute | solution.py:137
  19.3 5.7 %copy-start.4 = (bf16[256,1536]{1,0:T(8,128)(2,1)S(1)}, bf16[256,1536]{1,0:T(8,128)(2,1)}, u32[]{:S(2)}) copy-start(bf16[256,1536]{1,0:T(8,128)(2,1)} %param.7) | copy-start | bytes 2359300
  24.9 12.8 %copy-start.5 = (bf16[64,1024]{1,0:T(8,128)(2,1)S(1)}, bf16[64,1024]{1,0:T(8,128)(2,1)}, u32[]{:S(2)}) copy-start(bf16[64,1024]{1,0:T(8,128)(2,1)} %get-tuple-element.8) | copy-start | bytes 393220
  26.3 15.9 %copy-start.1 = (bf16[256,2048]{1,0:T(8,128)(2,1)S(1)}, bf16[256,2048]{1,0:T(8,128)(2,1)}, u32[]{:S(2)}) copy-start(bf16[256,2048]{1,0:T(8,128)(2,1)} %copy-done) | copy-start | bytes 3145732
  26.3 17.5 %copy-start.2 = (bf16[256,2048]{1,0:T(8,128)(2,1)S(1)}, bf16[256,2048]{1,0:T(8,128)(2,1)}, u32[]{:S(2)}) copy-start(bf16[256,2048]{1,0:T(8,128)(2,1)} %fusion.8) | copy-start | bytes 3145732
  26.3 17.4 %collective-permute-start.2 = (bf16[2,64,2048]{2,1,0:T(8,128)(2,1)S(1)}, bf16[2,64,2048]{2,1,0:T(8,128)(2,1)S(1)}, u32[]{:S(2)}, u32[]{:S(2)}) collective-permute-start(bf16[2,64,2048]{2,1,0:T(8,128)(2,1)S(1)} %pad_maximum_fusion.1), channel_id=1, source_target_pairs={{0,2},{1,3},{2,0},{3,1},{4,6},{5,7},{6,4},{7,5},{8,10},{9,11},{10,... | collective-permute-start | bytes 1572872 | tf_op jit(solution)/shard_map/ppermute | solution.py:137
  38.7 14.9 %collective-permute-start.7 = (bf16[4,64,1024]{2,1,0:T(8,128)(2,1)S(1)}, bf16[4,64,1024]{2,1,0:T(8,128)(2,1)S(1)}, u32[]{:S(2)}, u32[]{:S(2)}) collective-permute-start(bf16[4,64,1024]{2,1,0:T(8,128)(2,1)S(1)} %pad_maximum_fusion.3), channel_id=1, source_target_pairs={{0,1},{1,0},{2,3},{3,2},{4,5},{5,4},{6,7},{7,6},{8,9},{9,8},{10,11... | collective-permute-start | bytes 1572872 | tf_op jit(solution)/shard_map/ppermute | solution.py:104
  40.2 14.9 %collective-permute-start.8 = (bf16[4,64,1024]{2,1,0:T(8,128)(2,1)S(1)}, bf16[4,64,1024]{2,1,0:T(8,128)(2,1)S(1)}, u32[]{:S(2)}, u32[]{:S(2)}) collective-permute-start(bf16[4,64,1024]{2,1,0:T(8,128)(2,1)S(1)} %pad_maximum_fusion.3), channel_id=1, source_target_pairs={{0,2},{1,3},{2,0},{3,1},{4,6},{5,7},{6,4},{7,5},{8,10},{9,11},{10,... | collective-permute-start | bytes 1572872 | tf_op jit(solution)/shard_map/ppermute | solution.py:104
  43.2 49.7 %collective-permute-start.1 = (bf16[1,64,2048]{2,1,0:T(8,128)(2,1)S(1)}, bf16[1,64,2048]{2,1,0:T(8,128)(2,1)S(1)}, u32[]{:S(2)}, u32[]{:S(2)}) collective-permute-start(bf16[1,64,2048]{2,1,0:T(8,128)(2,1)S(1)} %fusion.21), channel_id=1, source_target_pairs={{0,2},{1,3},{2,0},{3,1},{4,6},{5,7},{6,4},{7,5},{8,10},{9,11},{10,... | collective-permute-start | bytes 786440 | tf_op jit(solution)/shard_map/ppermute | solution.py:137
  43.8 50.1 %collective-permute-start.3 = (bf16[1,64,2048]{2,1,0:T(8,128)(2,1)S(1)}, bf16[1,64,2048]{2,1,0:T(8,128)(2,1)S(1)}, u32[]{:S(2)}, u32[]{:S(2)}) collective-permute-start(bf16[1,64,2048]{2,1,0:T(8,128)(2,1)S(1)} %fusion.22), channel_id=1, source_target_pairs={{0,1},{1,0},{2,3},{3,2},{4,5},{5,4},{6,7},{7,6},{8,9},{9,8},{10,11... | collective-permute-start | bytes 786440 | tf_op jit(solution)/shard_map/ppermute | solution.py:137
  53.6 11.5 %collective-permute-start.9 = (bf16[2,64,1024]{2,1,0:T(8,128)(2,1)S(1)}, bf16[2,64,1024]{2,1,0:T(8,128)(2,1)S(1)}, u32[]{:S(2)}, u32[]{:S(2)}) collective-permute-start(bf16[2,64,1024]{2,1,0:T(8,128)(2,1)S(1)} %slice.121), channel_id=1, source_target_pairs={{0,2},{1,3},{2,0},{3,1},{4,6},{5,7},{6,4},{7,5},{8,10},{9,11},{10,... | collective-permute-start | bytes 786440 | tf_op jit(solution)/shard_map/ppermute | solution.py:106
  55.2 9.9 %collective-permute-start.10 = (bf16[2,64,1024]{2,1,0:T(8,128)(2,1)S(1)}, bf16[2,64,1024]{2,1,0:T(8,128)(2,1)S(1)}, u32[]{:S(2)}, u32[]{:S(2)}) collective-permute-start(bf16[2,64,1024]{2,1,0:T(8,128)(2,1)S(1)} %slice.124), channel_id=1, source_target_pairs={{0,1},{1,0},{2,3},{3,2},{4,5},{5,4},{6,7},{7,6},{8,9},{9,8},{10,11... | collective-permute-start | bytes 786440 | tf_op jit(solution)/shard_map/ppermute | solution.py:107
  58.1 9.1 %collective-permute-start.12 = (bf16[128,1536]{1,0:T(8,128)(2,1)S(1)}, bf16[128,1536]{1,0:T(8,128)(2,1)S(1)}, u32[]{:S(2)}, u32[]{:S(2)}) collective-permute-start(bf16[128,1536]{1,0:T(8,128)(2,1)S(1)} %get-tuple-element.19), channel_id=1, source_target_pairs={{0,16},{4,20},{16,24},{20,28},{24,8},{28,12},{8,0},{12,4},{1,17},{... | collective-permute-start | bytes 1179656 | tf_op jit(solution)/shard_map/ppermute | solution.py:93
  65.0 12.0 %collective-permute-start.13 = (bf16[128,1536]{1,0:T(8,128)(2,1)S(1)}, bf16[128,1536]{1,0:T(8,128)(2,1)S(1)}, u32[]{:S(2)}, u32[]{:S(2)}) collective-permute-start(bf16[128,1536]{1,0:T(8,128)(2,1)S(1)} %get-tuple-element.18), channel_id=1, source_target_pairs={{0,16},{4,20},{16,24},{20,28},{24,8},{28,12},{8,0},{12,4},{1,17},{... | collective-permute-start | bytes 1179656 | tf_op jit(solution)/shard_map/ppermute | solution.py:93
  67.2 18.3 %collective-permute-start.14 = (bf16[128,1536]{1,0:T(8,128)(2,1)S(1)}, bf16[128,1536]{1,0:T(8,128)(2,1)S(1)}, u32[]{:S(2)}, u32[]{:S(2)}) collective-permute-start(bf16[128,1536]{1,0:T(8,128)(2,1)S(1)} %collective-permute-done.12), channel_id=1, source_target_pairs={{0,16},{4,20},{16,24},{20,28},{24,8},{28,12},{8,0},{12,4},{1,17},{... | collective-permute-start | bytes 1179656 | tf_op jit(solution)/shard_map/ppermute | solution.py:93
  77.0 15.1 %collective-permute-start.15 = (bf16[128,1536]{1,0:T(8,128)(2,1)S(1)}, bf16[128,1536]{1,0:T(8,128)(2,1)S(1)}, u32[]{:S(2)}, u32[]{:S(2)}) collective-permute-start(bf16[128,1536]{1,0:T(8,128)(2,1)S(1)} %collective-permute-done.13), channel_id=1, source_target_pairs={{0,16},{4,20},{16,24},{20,28},{24,8},{28,12},{8,0},{12,4},{1,17},{... | collective-permute-start | bytes 1179656 | tf_op jit(solution)/shard_map/ppermute | solution.py:93
  92.7 3.5 %collective-permute-start.16 = (bf16[512,1536]{1,0:T(8,128)(2,1)S(1)}, bf16[512,1536]{1,0:T(8,128)(2,1)S(1)}, u32[]{:S(2)}, u32[]{:S(2)}) collective-permute-start(bf16[512,1536]{1,0:T(8,128)(2,1)S(1)} %fusion.4), channel_id=1, source_target_pairs={{0,4},{4,0},{8,12},{12,8},{16,20},{20,16},{24,28},{28,24},{1,5},{5... | collective-permute-start | bytes 4718600 | tf_op jit(solution)/shard_map/ppermute | solution.py:151

commit v2 on v1

--- a/solution.py
+++ b/solution.py
@@ -144,13 +144,16 @@
     own, other = sides
     most = chips * tokens - half
     last = moving[1]
-    handed = tdot(other[:most], every[:most])
+    theirs = lax.ppermute(other[most:], "ctx", swap)
+    handed = tdot(other[:most], every[:most]).astype(jnp.bfloat16)
+    moved = lax.ppermute(handed, "ctx", swap)
+    own, handed = lax.optimization_barrier((own, handed))
     kept = tdot(own[:most], every[:most])
-    handed, kept = lax.optimization_barrier((handed, kept))
-    handed = (handed + tdot(other[most:], last)).astype(jnp.bfloat16)
-    handed = lax.ppermute(handed, "ctx", swap)
-    kept = lax.optimization_barrier(kept + tdot(own[most:], last))
-    grad_weight = (kept + handed.astype(jnp.float32)) * scale
+    kept = lax.optimization_barrier(kept)
+    swapped = lax.ppermute(last, "ctx", swap)
+    kept = kept + moved.astype(jnp.float32) + tdot(own[most:], last)
+    kept = lax.optimization_barrier(kept)
+    grad_weight = (kept + tdot(theirs, swapped)) * scale
     return (grad_input, grad_weight)
 
 

time: 98.7 us -> 104 us (1.054)
  waiting for transfers between devices: 46.5 us -> 51.1 us
  other arithmetic: 7.66 us -> 5.5 us
  matrix products: 15.4 us -> 17.1 us
    ppermute x4, waiting for transfers between devices: 21.1 us -> 25.4 us  [body(): moving[h] = lax.ppermute(moving[h], 'ctx', shift(1))]
    mul x1 -> x0, other arithmetic: 2.15 us -> none  [body(): grad_weight = (kept + handed.astype(jnp.float32)) * scale]
    dot_general x4, matrix products: 4.82 us -> 6.5 us  [tdot(): lax.dot_general(a, b, (((0,), (0,)), ((), ())), preferred_element_type=jn...]
  transfers between devices with their start and end apart: 17 -> 19, of which waited for: 8 -> 8; matrix products, arithmetic and copies ran while one was open for 25% -> 24% of each run, Pallas kernels for 0% -> 0%
where the time goes in v2:
time: 104 us; the launch traced here: 103 us
  waiting for transfers between devices  51.1 us (49%)
  starting transfers between devices  21.9 us (21%)
  matrix products  17.1 us (16%)
  other arithmetic  5.5 us (5%)
  local copies, waits for them, and re-layouts  4.02 us (4%)
  Pallas kernels  2.87 us (3%)
    ppermute x4, waiting for transfers between devices, body(): moving[h] = lax.ppermute(moving[h], 'ctx', shift(1))  25.4 us
    dot_general x2, matrix products, body(): lax.dot_general(grad_out, lax.slice_in_dim(weight, h * span, (h + 1) * sp...  10.6 us
    ppermute x3, waiting for transfers between devices, body(): pieces[step] = lax.ppermute(pieces[step], 'ctx', shift(step))  9.8 us
    ppermute x2, waiting for transfers between devices, body(): got[j] = lax.ppermute(pieces, 'tp', peers(j))  9.13 us
    dot_general x4, matrix products, tdot(): lax.dot_general(a, b, (((0,), (0,)), ((), ())), preferred_element_type=jn...  6.5 us
    ppermute x3, starting transfers between devices, body(): pieces[step] = lax.ppermute(pieces[step], 'ctx', shift(step))  6.2 us
    ppermute x1, waiting for transfers between devices, body(): first = lax.ppermute(got[1][:middle], 'tp', peers(2))  5.65 us
    ppermute x4, starting transfers between devices, body(): sent = lax.ppermute(sent, 'tp', peers(bit))  4.25 us
  transfers between devices with their start and end apart: 19, of which 8 were waited for; matrix products, arithmetic and copies ran while one was open for 24% of the time, Pallas kernels for 0%

profile of v2, /device:TPU:0, one launch (start us, length us, event | category | flops | bytes accessed | tf_op | source)
XLA Modules:
  0.0 103.3 jit_solution(3931044540077055744)
XLA Ops:
  0.6 2.9 %shard_map.59 = (bf16[64,1024]{1,0:T(8,128)(2,1)}, bf16[64,1024]{1,0:T(8,128)(2,1)}, bf16[64,1024]{1,0:T(8,128)(2,1)}, bf16[64,1024]{1,0:T(8,128)(2,1)}) custom-call(bf16[64,4096]{1,0:T(8,128)(2,1)} %codes_ref.1, s32[32,64]{1,0:T(8,128)} %bitcast.97), custom_call_target="tpu_custom_call" | custom-call | flops 524288 | bytes 1048576 | tf_op jit(solution)/shard_map/pallas_call | solution.py:43
  3.5 4.1 %collective-permute-start.4 = (bf16[64,1024]{1,0:T(8,128)(2,1)}, bf16[64,1024]{1,0:T(8,128)(2,1)S(1)}, u32[]{:S(2)}, u32[]{:S(2)}) collective-permute-start(bf16[64,1024]{1,0:T(8,128)(2,1)} %get-tuple-element.8), channel_id=1, source_target_pairs={{0,16},{4,20},{16,24},{20,28},{24,8},{28,12},{8,0},{12,4},{1,17},{... | collective-permute-start | bytes 393224 | tf_op jit(solution)/shard_map/ppermute | solution.py:99
  7.6 1.3 %collective-permute-start.5 = (bf16[64,1024]{1,0:T(8,128)(2,1)}, bf16[64,1024]{1,0:T(8,128)(2,1)S(1)}, u32[]{:S(2)}, u32[]{:S(2)}) collective-permute-start(bf16[64,1024]{1,0:T(8,128)(2,1)} %get-tuple-element.9), channel_id=1, source_target_pairs={{0,24},{4,28},{16,8},{20,12},{24,0},{28,4},{8,16},{12,20},{1,25},{... | collective-permute-start | bytes 393224 | tf_op jit(solution)/shard_map/ppermute | solution.py:99
  8.9 0.8 collective-permute-start.6
  9.7 2.1 %collective-permute-start.11 = (bf16[256,1536]{1,0:T(8,128)(2,1)}, bf16[256,1536]{1,0:T(8,128)(2,1)}, u32[]{:S(2)}, u32[]{:S(2)}) collective-permute-start(bf16[256,1536]{1,0:T(8,128)(2,1)} %param.7), channel_id=1, source_target_pairs={{0,16},{4,20},{16,24},{20,28},{24,8},{28,12},{8,0},{12,4},{1,17},{... | collective-permute-start | bytes 2359304 | tf_op jit(solution)/shard_map/ppermute | solution.py:88
  11.8 4.9 %fusion.5 = bf16[256,2048]{1,0:T(8,128)(2,1)S(1)} fusion(bf16[256,1536]{1,0:T(8,128)(2,1)} %param.7, bf16[4096,1536]{1,0:T(8,128)(2,1)} %param.6), kind=kOutput, calls=%fused_computation.8 | convolution fusion | flops 1611137024 | bytes 8126464 | tf_op jit(solution)/shard_map/dot_general | solution.py:127
  16.8 0.1 dynamic-slice_bitcast_fusion.3
  16.8 0.9 pad_maximum_fusion
  17.8 1.5 %collective-permute-start = (bf16[2,64,2048]{2,1,0:T(8,128)(2,1)}, bf16[2,64,2048]{2,1,0:T(8,128)(2,1)}, u32[]{:S(2)}, u32[]{:S(2)}) collective-permute-start(bf16[2,64,2048]{2,1,0:T(8,128)(2,1)} %pad_maximum_fusion), channel_id=1, source_target_pairs={{0,1},{1,0},{2,3},{3,2},{4,5},{5,4},{6,7},{7,6},{8,9},{9,8},{10,11... | collective-permute-start | bytes 1572872 | tf_op jit(solution)/shard_map/ppermute | solution.py:137
  19.3 5.6 %fusion.8 = bf16[256,2048]{1,0:T(8,128)(2,1)} fusion(bf16[256,1536]{1,0:T(8,128)(2,1)S(1)} %copy-done.3, bf16[4096,1536]{1,0:T(8,128)(2,1)} %param.6), kind=kOutput, calls=%fused_computation.9 | convolution fusion | flops 1611137024 | bytes 8126464 | tf_op jit(solution)/shard_map/dot_general | solution.py:127
  24.9 0.2 dynamic_update_slice.55
  25.2 1.1 %dynamic-slice_bitcast_fusion.1 = (bf16[1,64,2048]{2,1,0:T(8,128)(2,1)S(1)}, bf16[1,64,2048]{2,1,0:T(8,128)(2,1)S(1)}) fusion(bf16[256,2048]{1,0:T(8,128)(2,1)} %fusion.8, s32[]{:T(128)S(6)} %select_n.96, s32[]{:T(128)S(6)} %select_n.95), kind=kLoop, calls=%fused_computation.42 | loop fusion | bytes 1048584 | tf_op jit(solution)/shard_map/stack | solution.py:136
  26.3 0.0 copy-start.2
  26.3 0.1 pad_maximum_fusion.1
  26.3 0.0 collective-permute-done.4
  26.3 1.6 %collective-permute-start.2 = (bf16[2,64,2048]{2,1,0:T(8,128)(2,1)S(1)}, bf16[2,64,2048]{2,1,0:T(8,128)(2,1)S(1)}, u32[]{:S(2)}, u32[]{:S(2)}) collective-permute-start(bf16[2,64,2048]{2,1,0:T(8,128)(2,1)S(1)} %pad_maximum_fusion.1), channel_id=1, source_target_pairs={{0,2},{1,3},{2,0},{3,1},{4,6},{5,7},{6,4},{7,5},{8,10},{9,11},{10,... | collective-permute-start | bytes 1572872 | tf_op jit(solution)/shard_map/ppermute | solution.py:137
  27.9 0.0 collective-permute-done.5
  27.9 9.8 %collective-permute-done.6 = bf16[64,1024]{1,0:T(8,128)(2,1)} collective-permute-done((bf16[64,1024]{1,0:T(8,128)(2,1)}, bf16[64,1024]{1,0:T(8,128)(2,1)}, u32[]{:S(2)}, u32[]{:S(2)}) %collective-permute-start.6) | collective-permute-done | bytes 131104 | tf_op jit(solution)/shard_map/ppermute | solution.py:99
  37.7 1.0 pad_maximum_fusion.3
  38.7 1.6 %collective-permute-start.7 = (bf16[4,64,1024]{2,1,0:T(8,128)(2,1)S(1)}, bf16[4,64,1024]{2,1,0:T(8,128)(2,1)S(1)}, u32[]{:S(2)}, u32[]{:S(2)}) collective-permute-start(bf16[4,64,1024]{2,1,0:T(8,128)(2,1)S(1)} %pad_maximum_fusion.3), channel_id=1, source_target_pairs={{0,1},{1,0},{2,3},{3,2},{4,5},{5,4},{6,7},{7,6},{8,9},{9,8},{10,11... | collective-permute-start | bytes 1572872 | tf_op jit(solution)/shard_map/ppermute | solution.py:104
  40.3 1.5 %collective-permute-start.8 = (bf16[4,64,1024]{2,1,0:T(8,128)(2,1)S(1)}, bf16[4,64,1024]{2,1,0:T(8,128)(2,1)S(1)}, u32[]{:S(2)}, u32[]{:S(2)}) collective-permute-start(bf16[4,64,1024]{2,1,0:T(8,128)(2,1)S(1)} %pad_maximum_fusion.3), channel_id=1, source_target_pairs={{0,2},{1,3},{2,0},{3,1},{4,6},{5,7},{6,4},{7,5},{8,10},{9,11},{10,... | collective-permute-start | bytes 1572872 | tf_op jit(solution)/shard_map/ppermute | solution.py:104
  41.8 0.1 broadcast.6.clone
  41.9 0.1 bitcast_dynamic-update-slice_fusion.2
  42.0 0.1 broadcast.6.clone.1
  42.1 0.1 bitcast_dynamic-update-slice_fusion.5
  42.1 0.0 collective-permute-done
  42.2 1.0 fusion.20
  43.2 0.6 collective-permute-start.1
  43.7 0.0 collective-permute-done.2
  43.8 0.1 fusion.21
  43.8 0.6 collective-permute-start.3
  44.4 9.1 %collective-permute-done.7 = bf16[4,64,1024]{2,1,0:T(8,128)(2,1)S(1)} collective-permute-done((bf16[4,64,1024]{2,1,0:T(8,128)(2,1)S(1)}, bf16[4,64,1024]{2,1,0:T(8,128)(2,1)S(1)}, u32[]{:S(2)}, u32[]{:S(2)}) %collective-permute-start.7) | collective-permute-done | bytes 524320 | tf_op jit(solution)/shard_map/ppermute | solution.py:104
  53.6 1.6 %collective-permute-start.9 = (bf16[2,64,1024]{2,1,0:T(8,128)(2,1)S(1)}, bf16[2,64,1024]{2,1,0:T(8,128)(2,1)S(1)}, u32[]{:S(2)}, u32[]{:S(2)}) collective-permute-start(bf16[2,64,1024]{2,1,0:T(8,128)(2,1)S(1)} %slice.121), channel_id=1, source_target_pairs={{0,2},{1,3},{2,0},{3,1},{4,6},{5,7},{6,4},{7,5},{8,10},{9,11},{10,... | collective-permute-start | bytes 786440 | tf_op jit(solution)/shard_map/ppermute | solution.py:106
  55.2 0.0 collective-permute-done.8
  55.2 1.6 %collective-permute-start.10 = (bf16[2,64,1024]{2,1,0:T(8,128)(2,1)S(1)}, bf16[2,64,1024]{2,1,0:T(8,128)(2,1)S(1)}, u32[]{:S(2)}, u32[]{:S(2)}) collective-permute-start(bf16[2,64,1024]{2,1,0:T(8,128)(2,1)S(1)} %slice.124), channel_id=1, source_target_pairs={{0,1},{1,0},{2,3},{3,2},{4,5},{5,4},{6,7},{7,6},{8,9},{9,8},{10,11... | collective-permute-start | bytes 786440 | tf_op jit(solution)/shard_map/ppermute | solution.py:107
  56.7 0.1 bitcast_dynamic-update-slice_fusion.1
  56.9 0.1 bitcast_dynamic-update-slice_fusion
  57.0 0.0 collective-permute-done.11
  57.0 1.2 %fusion.23 = (bf16[128,1536]{1,0:T(8,128)(2,1)S(1)}, bf16[128,1536]{1,0:T(8,128)(2,1)S(1)}) fusion(bf16[256,1536]{1,0:T(8,128)(2,1)} %collective-permute-done.11), kind=kLoop, calls=%fused_computation.54 | loop fusion | bytes 1572864 | tf_op jit(solution)/shard_map/slice | solution.py:90
  58.2 0.1 collective-permute-start.12
  58.2 1.2 %constant_dynamic-update-slice_fusion.3 = bf16[1024,1536]{1,0:T(8,128)(2,1)S(1)} fusion(bf16[1024,1536]{1,0:T(8,128)(2,1)S(1)} %dynamic_update_slice.55, bf16[256,1536]{1,0:T(8,128)(2,1)} %collective-permute-done.11), kind=kLoop, calls=%fused_computation.53 | loop fusion | bytes 1572864 | tf_op jit(solution)/shard_map/dynamic_update_slice | solution.py:89
  59.4 5.6 %collective-permute-done.9 = bf16[2,64,1024]{2,1,0:T(8,128)(2,1)S(1)} collective-permute-done((bf16[2,64,1024]{2,1,0:T(8,128)(2,1)S(1)}, bf16[2,64,1024]{2,1,0:T(8,128)(2,1)S(1)}, u32[]{:S(2)}, u32[]{:S(2)}) %collective-permute-start.9) | collective-permute-done | bytes 262176 | tf_op jit(solution)/shard_map/ppermute | solution.py:106
  65.1 0.0 collective-permute-done.10
  65.1 0.1 bitcast_dynamic-update-slice_fusion.6
  65.2 2.0 %collective-permute-done.12 = bf16[128,1536]{1,0:T(8,128)(2,1)S(1)} collective-permute-done((bf16[128,1536]{1,0:T(8,128)(2,1)S(1)}, bf16[128,1536]{1,0:T(8,128)(2,1)S(1)}, u32[]{:S(2)}, u32[]{:S(2)}) %collective-permute-start.12) | collective-permute-done | bytes 393248 | tf_op jit(solution)/shard_map/ppermute | solution.py:93
  67.2 1.2 %collective-permute-start.14 = (bf16[128,1536]{1,0:T(8,128)(2,1)S(1)}, bf16[128,1536]{1,0:T(8,128)(2,1)S(1)}, u32[]{:S(2)}, u32[]{:S(2)}) collective-permute-start(bf16[128,1536]{1,0:T(8,128)(2,1)S(1)} %collective-permute-done.12), channel_id=1, source_target_pairs={{0,16},{4,20},{16,24},{20,28},{24,8},{28,12},{8,0},{12,4},{1,17},{... | collective-permute-start | bytes 1179656 | tf_op jit(solution)/shard_map/ppermute | solution.py:93
  68.4 8.6 %collective-permute-done.13 = bf16[128,1536]{1,0:T(8,128)(2,1)S(1)} collective-permute-done((bf16[128,1536]{1,0:T(8,128)(2,1)S(1)}, bf16[128,1536]{1,0:T(8,128)(2,1)S(1)}, u32[]{:S(2)}, u32[]{:S(2)}) %collective-permute-start.13) | collective-permute-done | bytes 393248 | tf_op jit(solution)/shard_map/ppermute | solution.py:93
  77.1 6.7 %collective-permute-done.14 = bf16[128,1536]{1,0:T(8,128)(2,1)S(1)} collective-permute-done((bf16[128,1536]{1,0:T(8,128)(2,1)S(1)}, bf16[128,1536]{1,0:T(8,128)(2,1)S(1)}, u32[]{:S(2)}, u32[]{:S(2)}) %collective-permute-start.14) | collective-permute-done | bytes 393248 | tf_op jit(solution)/shard_map/ppermute | solution.py:93
  83.8 1.8 %convolution_convert_fusion = bf16[512,1536]{1,0:T(8,128)(2,1)S(1)} fusion(bf16[1024,1536]{1,0:T(8,128)(2,1)S(1)} %constant_dynamic-update-slice_fusion, bf16[1024,512]{1,0:T(8,128)(2,1)S(1)} %bitcast.92), kind=kOutput, calls=%fused_computation.7 | convolution fusion | flops 1410072576 | bytes 5242880 | tf_op jit(solution)/shard_map/dot_general | solution.py:55
  85.6 0.1 collective-permute-start.15
  85.7 1.1 %fusion.18 = bf16[64,2048]{1,0:T(8,128)(2,1)S(1)} fusion(bf16[2,64,2048]{2,1,0:T(8,128)(2,1)} %collective-permute-done, bf16[1,64,2048]{2,1,0:T(8,128)(2,1)S(1)} %collective-permute-done.1, bf16[256,2048]{1,0:T(8,128)(2,1)S(1)} %copy-done.1, s32[]{:T(128)S(6)} %select_n.93), kind=kLoop, calls=%fused_computation.25 | loop fusion | flops 786432 | bytes 1048580 | tf_op jit(solution)/shard_map/convert_element_type | solution.py:59
  86.7 0.0 collective-permute-done.3
  86.7 0.1 fusion.16
  86.9 0.8 pad_maximum_fusion.2
  87.7 0.5 collective-permute-start.17
  88.2 1.2 %collective-permute-start.16 = (bf16[128,1536]{1,0:T(8,128)(2,1)S(1)}, bf16[128,1536]{1,0:T(8,128)(2,1)S(1)}, u32[]{:S(2)}, u32[]{:S(2)}) collective-permute-start(bf16[128,1536]{1,0:T(8,128)(2,1)S(1)} %collective-permute-done.13), channel_id=1, source_target_pairs={{0,16},{4,20},{16,24},{20,28},{24,8},{28,12},{8,0},{12,4},{1,17},{... | collective-permute-start | bytes 1179656 | tf_op jit(solution)/shard_map/ppermute | solution.py:93
  89.4 1.8 %fusion.11 = f32[512,1536]{1,0:T(8,128)S(1)} fusion(bf16[1024,1536]{1,0:T(8,128)(2,1)S(1)} %constant_dynamic-update-slice_fusion, bf16[1024,512]{1,0:T(8,128)(2,1)S(1)} %bitcast.90), kind=kOutput, calls=%fused_computation.10 | convolution fusion | flops 1409286144 | bytes 6815744 | tf_op jit(solution)/shard_map/dot_general | solution.py:55
  91.3 8.1 %collective-permute-done.16 = bf16[128,1536]{1,0:T(8,128)(2,1)S(1)} collective-permute-done((bf16[128,1536]{1,0:T(8,128)(2,1)S(1)}, bf16[128,1536]{1,0:T(8,128)(2,1)S(1)}, u32[]{:S(2)}, u32[]{:S(2)}) %collective-permute-start.16) | collective-permute-done | bytes 393248 | tf_op jit(solution)/shard_map/ppermute | solution.py:93
  99.3 0.0 collective-permute-start.18
  99.3 0.0 collective-permute-done.15
  99.3 0.6 convolution_add_fusion.1
  99.9 0.0 collective-permute-done.17
  100.0 1.1 %collective-permute-done.18 = bf16[128,1536]{1,0:T(8,128)(2,1)S(1)} collective-permute-done((bf16[128,1536]{1,0:T(8,128)(2,1)S(1)}, bf16[128,1536]{1,0:T(8,128)(2,1)S(1)}, u32[]{:S(2)}, u32[]{:S(2)}) %collective-permute-start.18) | collective-permute-done | bytes 393248 | tf_op jit(solution)/shard_map/ppermute | solution.py:153
  101.1 2.3 %fusion.4 = f32[512,1536]{1,0:T(8,128)} fusion(f32[512,1536]{1,0:T(8,128)S(1)} %convolution_add_fusion.1, bf16[128,512]{1,0:T(8,128)(2,1)S(1)} %collective-permute-done.17, bf16[128,1536]{1,0:T(8,128)(2,1)S(1)} %collective-permute-done.18), kind=kOutput, calls=%fused_computation.6 | convolution fusion | flops 202899456 | bytes 6815744 | tf_op jit(solution)/shard_map/dot_general | solution.py:55
  (20 shorter events, 0.2 us)
Async XLA Ops:
  3.5 22.8 %collective-permute-start.4 = (bf16[64,1024]{1,0:T(8,128)(2,1)}, bf16[64,1024]{1,0:T(8,128)(2,1)S(1)}, u32[]{:S(2)}, u32[]{:S(2)}) collective-permute-start(bf16[64,1024]{1,0:T(8,128)(2,1)} %get-tuple-element.8), channel_id=1, source_target_pairs={{0,16},{4,20},{16,24},{20,28},{24,8},{28,12},{8,0},{12,4},{1,17},{... | collective-permute-start | bytes 393224 | tf_op jit(solution)/shard_map/ppermute | solution.py:99
  7.6 20.4 %collective-permute-start.5 = (bf16[64,1024]{1,0:T(8,128)(2,1)}, bf16[64,1024]{1,0:T(8,128)(2,1)S(1)}, u32[]{:S(2)}, u32[]{:S(2)}) collective-permute-start(bf16[64,1024]{1,0:T(8,128)(2,1)} %get-tuple-element.9), channel_id=1, source_target_pairs={{0,24},{4,28},{16,8},{20,12},{24,0},{28,4},{8,16},{12,20},{1,25},{... | collective-permute-start | bytes 393224 | tf_op jit(solution)/shard_map/ppermute | solution.py:99
  8.9 28.8 %collective-permute-start.6 = (bf16[64,1024]{1,0:T(8,128)(2,1)}, bf16[64,1024]{1,0:T(8,128)(2,1)}, u32[]{:S(2)}, u32[]{:S(2)}) collective-permute-start(bf16[64,1024]{1,0:T(8,128)(2,1)} %get-tuple-element.10), channel_id=1, source_target_pairs={{0,8},{4,12},{16,0},{20,4},{24,16},{28,20},{8,24},{12,28},{1,9},{5... | collective-permute-start | bytes 393224 | tf_op jit(solution)/shard_map/ppermute | solution.py:99
  9.7 47.3 %collective-permute-start.11 = (bf16[256,1536]{1,0:T(8,128)(2,1)}, bf16[256,1536]{1,0:T(8,128)(2,1)}, u32[]{:S(2)}, u32[]{:S(2)}) collective-permute-start(bf16[256,1536]{1,0:T(8,128)(2,1)} %param.7), channel_id=1, source_target_pairs={{0,16},{4,20},{16,24},{20,28},{24,8},{28,12},{8,0},{12,4},{1,17},{... | collective-permute-start | bytes 2359304 | tf_op jit(solution)/shard_map/ppermute | solution.py:88
  11.8 7.4 %copy-start.3 = (bf16[256,1536]{1,0:T(8,128)(2,1)S(1)}, bf16[256,1536]{1,0:T(8,128)(2,1)}, u32[]{:S(2)}) copy-start(bf16[256,1536]{1,0:T(8,128)(2,1)} %param.7) | copy-start | bytes 2359300
  16.8 2.5 %copy-start = (bf16[256,2048]{1,0:T(8,128)(2,1)}, bf16[256,2048]{1,0:T(8,128)(2,1)S(1)}, u32[]{:S(2)}) copy-start(bf16[256,2048]{1,0:T(8,128)(2,1)S(1)} %fusion.5) | copy-start | bytes 3145732
  17.8 24.4 %collective-permute-start = (bf16[2,64,2048]{2,1,0:T(8,128)(2,1)}, bf16[2,64,2048]{2,1,0:T(8,128)(2,1)}, u32[]{:S(2)}, u32[]{:S(2)}) collective-permute-start(bf16[2,64,2048]{2,1,0:T(8,128)(2,1)} %pad_maximum_fusion), channel_id=1, source_target_pairs={{0,1},{1,0},{2,3},{3,2},{4,5},{5,4},{6,7},{7,6},{8,9},{9,8},{10,11... | collective-permute-start | bytes 1572872 | tf_op jit(solution)/shard_map/ppermute | solution.py:137
  19.3 5.7 %copy-start.4 = (bf16[256,1536]{1,0:T(8,128)(2,1)S(1)}, bf16[256,1536]{1,0:T(8,128)(2,1)}, u32[]{:S(2)}) copy-start(bf16[256,1536]{1,0:T(8,128)(2,1)} %param.7) | copy-start | bytes 2359300
  24.9 12.8 %copy-start.5 = (bf16[64,1024]{1,0:T(8,128)(2,1)S(1)}, bf16[64,1024]{1,0:T(8,128)(2,1)}, u32[]{:S(2)}) copy-start(bf16[64,1024]{1,0:T(8,128)(2,1)} %get-tuple-element.7) | copy-start | bytes 393220
  26.2 15.9 %copy-start.1 = (bf16[256,2048]{1,0:T(8,128)(2,1)S(1)}, bf16[256,2048]{1,0:T(8,128)(2,1)}, u32[]{:S(2)}) copy-start(bf16[256,2048]{1,0:T(8,128)(2,1)} %copy-done) | copy-start | bytes 3145732
  26.3 17.5 %copy-start.2 = (bf16[256,2048]{1,0:T(8,128)(2,1)S(1)}, bf16[256,2048]{1,0:T(8,128)(2,1)}, u32[]{:S(2)}) copy-start(bf16[256,2048]{1,0:T(8,128)(2,1)} %fusion.8) | copy-start | bytes 3145732
  26.3 17.4 %collective-permute-start.2 = (bf16[2,64,2048]{2,1,0:T(8,128)(2,1)S(1)}, bf16[2,64,2048]{2,1,0:T(8,128)(2,1)S(1)}, u32[]{:S(2)}, u32[]{:S(2)}) collective-permute-start(bf16[2,64,2048]{2,1,0:T(8,128)(2,1)S(1)} %pad_maximum_fusion.1), channel_id=1, source_target_pairs={{0,2},{1,3},{2,0},{3,1},{4,6},{5,7},{6,4},{7,5},{8,10},{9,11},{10,... | collective-permute-start | bytes 1572872 | tf_op jit(solution)/shard_map/ppermute | solution.py:137
  38.7 14.9 %collective-permute-start.7 = (bf16[4,64,1024]{2,1,0:T(8,128)(2,1)S(1)}, bf16[4,64,1024]{2,1,0:T(8,128)(2,1)S(1)}, u32[]{:S(2)}, u32[]{:S(2)}) collective-permute-start(bf16[4,64,1024]{2,1,0:T(8,128)(2,1)S(1)} %pad_maximum_fusion.3), channel_id=1, source_target_pairs={{0,1},{1,0},{2,3},{3,2},{4,5},{5,4},{6,7},{7,6},{8,9},{9,8},{10,11... | collective-permute-start | bytes 1572872 | tf_op jit(solution)/shard_map/ppermute | solution.py:104
  40.3 14.9 %collective-permute-start.8 = (bf16[4,64,1024]{2,1,0:T(8,128)(2,1)S(1)}, bf16[4,64,1024]{2,1,0:T(8,128)(2,1)S(1)}, u32[]{:S(2)}, u32[]{:S(2)}) collective-permute-start(bf16[4,64,1024]{2,1,0:T(8,128)(2,1)S(1)} %pad_maximum_fusion.3), channel_id=1, source_target_pairs={{0,2},{1,3},{2,0},{3,1},{4,6},{5,7},{6,4},{7,5},{8,10},{9,11},{10,... | collective-permute-start | bytes 1572872 | tf_op jit(solution)/shard_map/ppermute | solution.py:104
  43.2 42.5 %collective-permute-start.1 = (bf16[1,64,2048]{2,1,0:T(8,128)(2,1)S(1)}, bf16[1,64,2048]{2,1,0:T(8,128)(2,1)S(1)}, u32[]{:S(2)}, u32[]{:S(2)}) collective-permute-start(bf16[1,64,2048]{2,1,0:T(8,128)(2,1)S(1)} %fusion.20), channel_id=1, source_target_pairs={{0,2},{1,3},{2,0},{3,1},{4,6},{5,7},{6,4},{7,5},{8,10},{9,11},{10,... | collective-permute-start | bytes 786440 | tf_op jit(solution)/shard_map/ppermute | solution.py:137
  43.8 42.9 %collective-permute-start.3 = (bf16[1,64,2048]{2,1,0:T(8,128)(2,1)S(1)}, bf16[1,64,2048]{2,1,0:T(8,128)(2,1)S(1)}, u32[]{:S(2)}, u32[]{:S(2)}) collective-permute-start(bf16[1,64,2048]{2,1,0:T(8,128)(2,1)S(1)} %fusion.21), channel_id=1, source_target_pairs={{0,1},{1,0},{2,3},{3,2},{4,5},{5,4},{6,7},{7,6},{8,9},{9,8},{10,11... | collective-permute-start | bytes 786440 | tf_op jit(solution)/shard_map/ppermute | solution.py:137
  53.6 11.5 %collective-permute-start.9 = (bf16[2,64,1024]{2,1,0:T(8,128)(2,1)S(1)}, bf16[2,64,1024]{2,1,0:T(8,128)(2,1)S(1)}, u32[]{:S(2)}, u32[]{:S(2)}) collective-permute-start(bf16[2,64,1024]{2,1,0:T(8,128)(2,1)S(1)} %slice.121), channel_id=1, source_target_pairs={{0,2},{1,3},{2,0},{3,1},{4,6},{5,7},{6,4},{7,5},{8,10},{9,11},{10,... | collective-permute-start | bytes 786440 | tf_op jit(solution)/shard_map/ppermute | solution.py:106
  55.2 9.9 %collective-permute-start.10 = (bf16[2,64,1024]{2,1,0:T(8,128)(2,1)S(1)}, bf16[2,64,1024]{2,1,0:T(8,128)(2,1)S(1)}, u32[]{:S(2)}, u32[]{:S(2)}) collective-permute-start(bf16[2,64,1024]{2,1,0:T(8,128)(2,1)S(1)} %slice.124), channel_id=1, source_target_pairs={{0,1},{1,0},{2,3},{3,2},{4,5},{5,4},{6,7},{7,6},{8,9},{9,8},{10,11... | collective-permute-start | bytes 786440 | tf_op jit(solution)/shard_map/ppermute | solution.py:107
  58.2 9.1 %collective-permute-start.12 = (bf16[128,1536]{1,0:T(8,128)(2,1)S(1)}, bf16[128,1536]{1,0:T(8,128)(2,1)S(1)}, u32[]{:S(2)}, u32[]{:S(2)}) collective-permute-start(bf16[128,1536]{1,0:T(8,128)(2,1)S(1)} %get-tuple-element.16), channel_id=1, source_target_pairs={{0,16},{4,20},{16,24},{20,28},{24,8},{28,12},{8,0},{12,4},{1,17},{... | collective-permute-start | bytes 1179656 | tf_op jit(solution)/shard_map/ppermute | solution.py:93
  65.1 12.0 %collective-permute-start.13 = (bf16[128,1536]{1,0:T(8,128)(2,1)S(1)}, bf16[128,1536]{1,0:T(8,128)(2,1)S(1)}, u32[]{:S(2)}, u32[]{:S(2)}) collective-permute-start(bf16[128,1536]{1,0:T(8,128)(2,1)S(1)} %get-tuple-element.17), channel_id=1, source_target_pairs={{0,16},{4,20},{16,24},{20,28},{24,8},{28,12},{8,0},{12,4},{1,17},{... | collective-permute-start | bytes 1179656 | tf_op jit(solution)/shard_map/ppermute | solution.py:93
  67.2 16.5 %collective-permute-start.14 = (bf16[128,1536]{1,0:T(8,128)(2,1)S(1)}, bf16[128,1536]{1,0:T(8,128)(2,1)S(1)}, u32[]{:S(2)}, u32[]{:S(2)}) collective-permute-start(bf16[128,1536]{1,0:T(8,128)(2,1)S(1)} %collective-permute-done.12), channel_id=1, source_target_pairs={{0,16},{4,20},{16,24},{20,28},{24,8},{28,12},{8,0},{12,4},{1,17},{... | collective-permute-start | bytes 1179656 | tf_op jit(solution)/shard_map/ppermute | solution.py:93
  85.6 13.8 %collective-permute-start.15 = (bf16[512,1536]{1,0:T(8,128)(2,1)S(1)}, bf16[512,1536]{1,0:T(8,128)(2,1)S(1)}, u32[]{:S(2)}, u32[]{:S(2)}) collective-permute-start(bf16[512,1536]{1,0:T(8,128)(2,1)S(1)} %convolution_convert_fusion), channel_id=1, source_target_pairs={{0,4},{4,0},{8,12},{12,8},{16,20},{20,16},{24,28},{28,24},{1,5},{5... | collective-permute-start | bytes 4718600 | tf_op jit(solution)/shard_map/ppermute | solution.py:149
  87.7 12.2 %collective-permute-start.17 = (bf16[128,512]{1,0:T(8,128)(2,1)S(1)}, bf16[128,512]{1,0:T(8,128)(2,1)S(1)}, u32[]{:S(2)}, u32[]{:S(2)}) collective-permute-start(bf16[128,512]{1,0:T(8,128)(2,1)S(1)} %slice.131), channel_id=1, source_target_pairs={{0,4},{4,0},{8,12},{12,8},{16,20},{20,16},{24,28},{28,24},{1,5},{5... | collective-permute-start | bytes 393224 | tf_op jit(solution)/shard_map/ppermute | solution.py:147
  88.2 11.1 %collective-permute-start.16 = (bf16[128,1536]{1,0:T(8,128)(2,1)S(1)}, bf16[128,1536]{1,0:T(8,128)(2,1)S(1)}, u32[]{:S(2)}, u32[]{:S(2)}) collective-permute-start(bf16[128,1536]{1,0:T(8,128)(2,1)S(1)} %collective-permute-done.13), channel_id=1, source_target_pairs={{0,16},{4,20},{16,24},{20,28},{24,8},{28,12},{8,0},{12,4},{1,17},{... | collective-permute-start | bytes 1179656 | tf_op jit(solution)/shard_map/ppermute | solution.py:93
  99.3 1.7 %collective-permute-start.18 = (bf16[128,1536]{1,0:T(8,128)(2,1)S(1)}, bf16[128,1536]{1,0:T(8,128)(2,1)S(1)}, u32[]{:S(2)}, u32[]{:S(2)}) collective-permute-start(bf16[128,1536]{1,0:T(8,128)(2,1)S(1)} %collective-permute-done.16), channel_id=1, source_target_pairs={{0,4},{4,0},{8,12},{12,8},{16,20},{20,16},{24,28},{28,24},{1,5},{5... | collective-permute-start | bytes 1179656 | tf_op jit(solution)/shard_map/ppermute | solution.py:153

commit v3 on v2

--- a/solution.py
+++ b/solution.py
@@ -51,6 +51,54 @@
     )(codes, exponents.T)
 
 
+def finish_kernel(count, at, part_ref, more_ref, *refs):
+    out_ref, ready_ref, sems = refs[-3:]
+    wide = part_ref.shape[1]
+    step = wide // sems.shape[0]
+    scale = lax.rsqrt(jnp.full((1, step), count, jnp.float32))
+    copies = []
+    for n in range(sems.shape[0]):
+        cut = slice(n * step, (n + 1) * step)
+        if len(refs) == 3:
+            more = more_ref[:, cut].astype(jnp.float32)
+        else:
+            more = tdot(more_ref[...], refs[0][:, cut])
+        ready_ref[:, cut] = (part_ref[:, cut] + more) * scale
+        place = out_ref.at[:, at * wide + n * step : at * wide + (n + 1) * step]
+        copies.append(pltpu.make_async_copy(ready_ref.at[:, cut], place, sems.at[n]))
+        copies[-1].start()
+    for copy in copies:
+        copy.wait()
+
+
+def finish(part, more, swapped, before, count, columns):
+    rows, wide = part.shape
+    if wide % 128:
+        more = more.astype(jnp.float32) if swapped is None else tdot(more, swapped)
+        part = (part + more) * lax.rsqrt(jnp.float32(count))
+        return part if before is None else jnp.concatenate([before, part], axis=1)
+    at = 0 if before is None else 1
+    operands = [part, more] + ([] if before is None else [swapped, before])
+    specs = [VMEM] * min(3, len(operands))
+    if before is not None:
+        specs.append(pl.BlockSpec(memory_space=pl.ANY))
+    return pl.pallas_call(
+        functools.partial(finish_kernel, count, at),
+        out_shape=jax.ShapeDtypeStruct((rows, columns), jnp.float32),
+        in_specs=specs,
+        out_specs=pl.BlockSpec(memory_space=pl.ANY),
+        scratch_shapes=[
+            pltpu.VMEM((rows, wide), jnp.float32),
+            pltpu.SemaphoreType.DMA((wide // 128 // (2 - wide // 128 % 2),)),
+        ],
+        input_output_aliases={} if before is None else {3: 0},
+        compiler_params=pltpu.CompilerParams(vmem_limit_bytes=8 << 20),
+        cost_estimate=pl.CostEstimate(
+            flops=2 * rows * wide * 256, bytes_accessed=4 * rows * wide, transcendentals=0
+        ),
+    )(*operands)
+
+
 def tdot(a, b):
     return lax.dot_general(a, b, (((0,), (0,)), ((), ())), preferred_element_type=jnp.float32)
 
@@ -69,7 +117,6 @@
     out_rows = width // n_ctx
     core = lax.axis_index("ctx") % 2
     order = ring_order(chips)
-    half = tokens // 2
 
     swap = [(i, i ^ 1) for i in range(n_ctx)]
 
@@ -83,16 +130,22 @@
     def peers(j):
         return [(i, i ^ j) for i in range(n_tp)]
 
-    every = jnp.zeros((chips * tokens, grad_out.shape[1]), jnp.bfloat16)
-    every = lax.dynamic_update_slice(every, grad_out, (0, 0))
+    columns = grad_out.shape[1]
+    ends = (0, columns // 2, columns)
+    every = []
+    for h in range(2):
+        size = (chips - h) * tokens
+        block = jnp.zeros((size, ends[h + 1] - ends[h]), jnp.bfloat16)
+        every.append(lax.dynamic_update_slice(block, grad_out[:, ends[h] : ends[h + 1]], (0, 0)))
     moving = lax.ppermute(grad_out, "ctx", shift(1))
-    every = lax.dynamic_update_slice(every, moving, (tokens, 0))
-    moving = [moving[:half], moving[half:]]
+    moving = [moving[:, ends[h] : ends[h + 1]] for h in range(2)]
+    for h in range(2):
+        every[h] = lax.dynamic_update_slice(every[h], moving[h], (tokens, 0))
     for step in range(2, chips):
         for h in range(2):
             moving[h] = lax.ppermute(moving[h], "ctx", shift(1))
             if step < chips - 1 or h == 0:
-                every = lax.dynamic_update_slice(every, moving[h], (step * tokens + h * half, 0))
+                every[h] = lax.dynamic_update_slice(every[h], moving[h], (step * tokens, 0))
 
     pieces = list(prepare(act_codes, scale_exps, order))
     for step in range(1, chips):
@@ -140,20 +193,21 @@
         outs.append(added(held[0]))
     grad_input = jnp.concatenate(outs, axis=1)
 
-    scale = lax.rsqrt(jnp.float32(tokens * n_ctx))
+    scale_of = tokens * n_ctx
     own, other = sides
-    most = chips * tokens - half
+    most = (chips - 1) * tokens
     last = moving[1]
     theirs = lax.ppermute(other[most:], "ctx", swap)
-    handed = tdot(other[:most], every[:most]).astype(jnp.bfloat16)
-    moved = lax.ppermute(handed, "ctx", swap)
-    own, handed = lax.optimization_barrier((own, handed))
-    kept = tdot(own[:most], every[:most])
-    kept = lax.optimization_barrier(kept)
+    handed, kept = [], []
+    for h, depth in enumerate((chips * tokens, most)):
+        product = tdot(other[:depth], every[h]).astype(jnp.bfloat16)
+        handed.append(lax.ppermute(product, "ctx", swap))
+    for h, depth in enumerate((chips * tokens, most)):
+        kept.append(lax.optimization_barrier(tdot(own[:depth], every[h])))
+    grad_weight = finish(kept[0], handed[0], None, None, scale_of, columns)
     swapped = lax.ppermute(last, "ctx", swap)
-    kept = kept + moved.astype(jnp.float32) + tdot(own[most:], last)
-    kept = lax.optimization_barrier(kept)
-    grad_weight = (kept + tdot(theirs, swapped)) * scale
+    rest = kept[1] + handed[1].astype(jnp.float32) + tdot(own[most:], last)
+    grad_weight = finish(rest, theirs, swapped, grad_weight, scale_of, columns)
     return (grad_input, grad_weight)
 
 

time: 104 us -> 102 us (0.981)
  waiting for transfers between devices: 51.1 us -> 47.7 us
  Pallas kernels: 2.87 us -> 5.52 us
  matrix products: 17.1 us -> 14.5 us
  starting transfers between devices: 21.9 us -> 24 us
    ppermute x1, waiting for transfers between devices: 5.65 us -> 0.01 us  [body(): first = lax.ppermute(got[1][:middle], 'tp', peers(2))]
    ppermute x4, waiting for transfers between devices: 0.01 us -> 3.7 us  [body(): sent = lax.ppermute(sent, 'tp', peers(bit))]
    pallas_call x0 -> x2, Pallas kernels: none -> 2.66 us  [finish(): pl.pallas_call(functools.partial(finish_kernel, count, at), out_shape=jax...]
    ppermute x4, starting transfers between devices: 2.43 us -> 4.95 us  [body(): moving[h] = lax.ppermute(moving[h], 'ctx', shift(1))]
    dot_general x4 -> x5, matrix products: 6.5 us -> 4.09 us  [tdot(): lax.dot_general(a, b, (((0,), (0,)), ((), ())), preferred_element_type=jn...]
    dynamic_update_slice x5, local copies, waits for them, and re-layouts: 1.47 us -> 0.26 us  [the longest x2 0.18 us: body(): lax.dynamic_update_slice(block, grad_out[:, ends[h]:ends[h + 1]], (0, 0))]
    ppermute x1, waiting for transfers between devices: 1.11 us -> 0.01 us  [body(): swapped = lax.ppermute(last, 'ctx', swap)]
  transfers between devices with their start and end apart: 19 -> 20, of which waited for: 8 -> 7; matrix products, arithmetic and copies ran while one was open for 24% -> 22% of each run, Pallas kernels for 0% -> 1%
where the time goes in v3:
time: 102 us
  waiting for transfers between devices  47.7 us (47%)
  starting transfers between devices  24 us (24%)
  matrix products  14.5 us (14%)
  Pallas kernels  5.52 us (5%)
  other arithmetic  5.38 us (5%)
  local copies, waits for them, and re-layouts  3.98 us (4%)
  between operations  1.03 us (1%)
    ppermute x4, waiting for transfers between devices, body(): moving[h] = lax.ppermute(moving[h], 'ctx', shift(1))  25.7 us
    dot_general x2, matrix products, body(): lax.dot_general(grad_out, lax.slice_in_dim(weight, h * span, (h + 1) * sp...  10.4 us
    ppermute x3, waiting for transfers between devices, body(): pieces[step] = lax.ppermute(pieces[step], 'ctx', shift(step))  10 us
    ppermute x2, waiting for transfers between devices, body(): got[j] = lax.ppermute(pieces, 'tp', peers(j))  8.19 us
    ppermute x3, starting transfers between devices, body(): pieces[step] = lax.ppermute(pieces[step], 'ctx', shift(step))  6.2 us
    ppermute x4, starting transfers between devices, body(): moving[h] = lax.ppermute(moving[h], 'ctx', shift(1))  4.95 us
    ppermute x4, starting transfers between devices, body(): sent = lax.ppermute(sent, 'tp', peers(bit))  4.25 us
    dot_general x5, matrix products, tdot(): lax.dot_general(a, b, (((0,), (0,)), ((), ())), preferred_element_type=jn...  4.09 us
  transfers between devices with their start and end apart: 20, of which 7 were waited for; matrix products, arithmetic and copies ran while one was open for 22% of the time, Pallas kernels for 1%

profile of v3, /device:TPU:0, one launch (start us, length us, event | category | flops | bytes accessed | tf_op | source)
XLA Modules:
  0.0 102.1 jit_solution(701642950398293661)
XLA Ops:
  0.6 2.9 %shard_map.59 = (bf16[64,1024]{1,0:T(8,128)(2,1)}, bf16[64,1024]{1,0:T(8,128)(2,1)}, bf16[64,1024]{1,0:T(8,128)(2,1)}, bf16[64,1024]{1,0:T(8,128)(2,1)}) custom-call(bf16[64,4096]{1,0:T(8,128)(2,1)} %codes_ref.1, s32[32,64]{1,0:T(8,128)} %bitcast.110), custom_call_target="tpu_custom_call" | custom-call | flops 524288 | bytes 1048576 | tf_op jit(solution)/shard_map/pallas_call | solution.py:43
  3.5 4.1 %collective-permute-start.4 = (bf16[64,1024]{1,0:T(8,128)(2,1)}, bf16[64,1024]{1,0:T(8,128)(2,1)S(1)}, u32[]{:S(2)}, u32[]{:S(2)}) collective-permute-start(bf16[64,1024]{1,0:T(8,128)(2,1)} %get-tuple-element.7), channel_id=1, source_target_pairs={{0,16},{4,20},{16,24},{20,28},{24,8},{28,12},{8,0},{12,4},{1,17},{... | collective-permute-start | bytes 393224 | tf_op jit(solution)/shard_map/ppermute | solution.py:152
  7.6 1.3 %collective-permute-start.5 = (bf16[64,1024]{1,0:T(8,128)(2,1)}, bf16[64,1024]{1,0:T(8,128)(2,1)S(1)}, u32[]{:S(2)}, u32[]{:S(2)}) collective-permute-start(bf16[64,1024]{1,0:T(8,128)(2,1)} %get-tuple-element.8), channel_id=1, source_target_pairs={{0,24},{4,28},{16,8},{20,12},{24,0},{28,4},{8,16},{12,20},{1,25},{... | collective-permute-start | bytes 393224 | tf_op jit(solution)/shard_map/ppermute | solution.py:152
  8.9 0.8 collective-permute-start.6
  9.7 2.1 %collective-permute-start.11 = (bf16[256,1536]{1,0:T(8,128)(2,1)}, bf16[256,1536]{1,0:T(8,128)(2,1)}, u32[]{:S(2)}, u32[]{:S(2)}) collective-permute-start(bf16[256,1536]{1,0:T(8,128)(2,1)} %param.7), channel_id=1, source_target_pairs={{0,16},{4,20},{16,24},{20,28},{24,8},{28,12},{8,0},{12,4},{1,17},{... | collective-permute-start | bytes 2359304 | tf_op jit(solution)/shard_map/ppermute | solution.py:140
  11.8 4.9 %fusion.4 = bf16[256,2048]{1,0:T(8,128)(2,1)S(1)} fusion(bf16[256,1536]{1,0:T(8,128)(2,1)} %param.7, bf16[4096,1536]{1,0:T(8,128)(2,1)} %param.6), kind=kOutput, calls=%fused_computation.4 | convolution fusion | flops 1611137024 | bytes 8126464 | tf_op jit(solution)/shard_map/dot_general | solution.py:180
  16.7 0.0 copy-start.3
  16.8 0.8 pad_maximum_fusion
  17.6 1.5 %collective-permute-start = (bf16[2,64,2048]{2,1,0:T(8,128)(2,1)}, bf16[2,64,2048]{2,1,0:T(8,128)(2,1)}, u32[]{:S(2)}, u32[]{:S(2)}) collective-permute-start(bf16[2,64,2048]{2,1,0:T(8,128)(2,1)} %pad_maximum_fusion), channel_id=1, source_target_pairs={{0,1},{1,0},{2,3},{3,2},{4,5},{5,4},{6,7},{7,6},{8,9},{9,8},{10,11... | collective-permute-start | bytes 1572872 | tf_op jit(solution)/shard_map/ppermute | solution.py:190
  19.1 0.1 fusion.17
  19.2 5.6 %fusion.7 = bf16[256,2048]{1,0:T(8,128)(2,1)} fusion(bf16[256,1536]{1,0:T(8,128)(2,1)S(1)} %copy-done.3, bf16[4096,1536]{1,0:T(8,128)(2,1)} %param.6), kind=kOutput, calls=%fused_computation.5 | convolution fusion | flops 1611137024 | bytes 8126464 | tf_op jit(solution)/shard_map/dot_general | solution.py:180
  24.8 0.1 dynamic_update_slice.64
  24.9 0.1 dynamic_update_slice.56
  25.0 1.1 %dynamic-slice_bitcast_fusion.1 = (bf16[1,64,2048]{2,1,0:T(8,128)(2,1)S(1)}, bf16[1,64,2048]{2,1,0:T(8,128)(2,1)S(1)}) fusion(bf16[256,2048]{1,0:T(8,128)(2,1)} %fusion.7, s32[]{:T(128)S(6)} %select_n.96, s32[]{:T(128)S(6)} %select_n.95), kind=kLoop, calls=%fused_computation.36 | loop fusion | bytes 1048584 | tf_op jit(solution)/shard_map/stack | solution.py:189
  26.1 0.1 pad_maximum_fusion.1
  26.1 0.0 collective-permute-done.4
  26.1 1.6 %collective-permute-start.2 = (bf16[2,64,2048]{2,1,0:T(8,128)(2,1)S(1)}, bf16[2,64,2048]{2,1,0:T(8,128)(2,1)S(1)}, u32[]{:S(2)}, u32[]{:S(2)}) collective-permute-start(bf16[2,64,2048]{2,1,0:T(8,128)(2,1)S(1)} %pad_maximum_fusion.1), channel_id=1, source_target_pairs={{0,2},{1,3},{2,0},{3,1},{4,6},{5,7},{6,4},{7,5},{8,10},{9,11},{10,... | collective-permute-start | bytes 1572872 | tf_op jit(solution)/shard_map/ppermute | solution.py:190
  27.7 10.0 %collective-permute-done.6 = bf16[64,1024]{1,0:T(8,128)(2,1)} collective-permute-done((bf16[64,1024]{1,0:T(8,128)(2,1)}, bf16[64,1024]{1,0:T(8,128)(2,1)}, u32[]{:S(2)}, u32[]{:S(2)}) %collective-permute-start.6) | collective-permute-done | bytes 131104 | tf_op jit(solution)/shard_map/ppermute | solution.py:152
  37.7 1.0 pad_maximum_fusion.3
  38.7 1.6 %collective-permute-start.7 = (bf16[4,64,1024]{2,1,0:T(8,128)(2,1)S(1)}, bf16[4,64,1024]{2,1,0:T(8,128)(2,1)S(1)}, u32[]{:S(2)}, u32[]{:S(2)}) collective-permute-start(bf16[4,64,1024]{2,1,0:T(8,128)(2,1)S(1)} %pad_maximum_fusion.3), channel_id=1, source_target_pairs={{0,1},{1,0},{2,3},{3,2},{4,5},{5,4},{6,7},{7,6},{8,9},{9,8},{10,11... | collective-permute-start | bytes 1572872 | tf_op jit(solution)/shard_map/ppermute | solution.py:157
  40.2 1.5 %collective-permute-start.8 = (bf16[4,64,1024]{2,1,0:T(8,128)(2,1)S(1)}, bf16[4,64,1024]{2,1,0:T(8,128)(2,1)S(1)}, u32[]{:S(2)}, u32[]{:S(2)}) collective-permute-start(bf16[4,64,1024]{2,1,0:T(8,128)(2,1)S(1)} %pad_maximum_fusion.3), channel_id=1, source_target_pairs={{0,2},{1,3},{2,0},{3,1},{4,6},{5,7},{6,4},{7,5},{8,10},{9,11},{10,... | collective-permute-start | bytes 1572872 | tf_op jit(solution)/shard_map/ppermute | solution.py:157
  41.8 0.1 broadcast.8.clone
  41.9 0.0 copy-start.2
  41.9 0.1 bitcast_dynamic-update-slice_fusion.2
  42.0 0.1 broadcast.8.clone.1
  42.1 0.1 bitcast_dynamic-update-slice_fusion.5
  42.2 0.0 collective-permute-done
  42.2 0.9 copy-done.1
  43.1 1.0 fusion.14
  44.1 0.6 collective-permute-start.1
  44.7 0.1 fusion.15
  44.8 0.6 collective-permute-start.3
  45.4 8.2 %collective-permute-done.7 = bf16[4,64,1024]{2,1,0:T(8,128)(2,1)S(1)} collective-permute-done((bf16[4,64,1024]{2,1,0:T(8,128)(2,1)S(1)}, bf16[4,64,1024]{2,1,0:T(8,128)(2,1)S(1)}, u32[]{:S(2)}, u32[]{:S(2)}) %collective-permute-start.7) | collective-permute-done | bytes 524320 | tf_op jit(solution)/shard_map/ppermute | solution.py:157
  53.6 1.6 %collective-permute-start.9 = (bf16[2,64,1024]{2,1,0:T(8,128)(2,1)S(1)}, bf16[2,64,1024]{2,1,0:T(8,128)(2,1)S(1)}, u32[]{:S(2)}, u32[]{:S(2)}) collective-permute-start(bf16[2,64,1024]{2,1,0:T(8,128)(2,1)S(1)} %slice.140), channel_id=1, source_target_pairs={{0,2},{1,3},{2,0},{3,1},{4,6},{5,7},{6,4},{7,5},{8,10},{9,11},{10,... | collective-permute-start | bytes 786440 | tf_op jit(solution)/shard_map/ppermute | solution.py:159
  55.2 0.0 collective-permute-done.8
  55.2 1.6 %collective-permute-start.10 = (bf16[2,64,1024]{2,1,0:T(8,128)(2,1)S(1)}, bf16[2,64,1024]{2,1,0:T(8,128)(2,1)S(1)}, u32[]{:S(2)}, u32[]{:S(2)}) collective-permute-start(bf16[2,64,1024]{2,1,0:T(8,128)(2,1)S(1)} %slice.143), channel_id=1, source_target_pairs={{0,1},{1,0},{2,3},{3,2},{4,5},{5,4},{6,7},{7,6},{8,9},{9,8},{10,11... | collective-permute-start | bytes 786440 | tf_op jit(solution)/shard_map/ppermute | solution.py:160
  56.7 0.1 bitcast_dynamic-update-slice_fusion.1
  56.9 0.1 bitcast_dynamic-update-slice_fusion
  57.0 3.7 %collective-permute-done.1 = bf16[1,64,2048]{2,1,0:T(8,128)(2,1)S(1)} collective-permute-done((bf16[1,64,2048]{2,1,0:T(8,128)(2,1)S(1)}, bf16[1,64,2048]{2,1,0:T(8,128)(2,1)S(1)}, u32[]{:S(2)}, u32[]{:S(2)}) %collective-permute-start.1) | collective-permute-done | bytes 262176 | tf_op jit(solution)/shard_map/ppermute | solution.py:190
  60.7 1.1 %fusion.12 = bf16[64,2048]{1,0:T(8,128)(2,1)S(1)} fusion(bf16[2,64,2048]{2,1,0:T(8,128)(2,1)} %collective-permute-done, bf16[1,64,2048]{2,1,0:T(8,128)(2,1)S(1)} %collective-permute-done.1, bf16[256,2048]{1,0:T(8,128)(2,1)S(1)} %copy-done.1, s32[]{:T(128)S(6)} %select_n.93), kind=kLoop, calls=%fused_computation.19 | loop fusion | flops 786432 | bytes 1048580 | tf_op jit(solution)/shard_map/convert_element_type | solution.py:107
  61.7 0.1 fusion.10
  61.8 0.8 pad_maximum_fusion.2
  62.7 1.2 %fusion.16 = (bf16[256,768]{1,0:T(8,128)(2,1)S(1)}, bf16[768,768]{1,0:T(8,128)(2,1)S(1)}, bf16[1024,768]{1,0:T(8,128)(2,1)S(1)}, bf16[256,768]{1,0:T(8,128)(2,1)S(1)}) fusion(bf16[256,1536]{1,0:T(8,128)(2,1)} %collective-permute-done.11, bf16[768,768]{1,0:T(8,128)(2,1)S(1)} %dynamic_update_slice.56, bf16[1024,768]{1,0:T(8,128)(2,1)S(1)} %dynamic_update_slice.64), kind=kLoop, calls=%fused_computation.48 | loop fusion | bytes 2359296 | tf_op jit(solution)/shard_map/slice | solution.py:141
  63.9 0.1 collective-permute-start.17
  64.0 3.0 %collective-permute-start.12 = (bf16[256,768]{1,0:T(8,128)(2,1)S(1)}, bf16[256,768]{1,0:T(8,128)(2,1)S(1)}, u32[]{:S(2)}, u32[]{:S(2)}) collective-permute-start(bf16[256,768]{1,0:T(8,128)(2,1)S(1)} %get-tuple-element.17), channel_id=1, source_target_pairs={{0,16},{4,20},{16,24},{20,28},{24,8},{28,12},{8,0},{12,4},{1,17},{... | collective-permute-start | bytes 1179656 | tf_op jit(solution)/shard_map/ppermute | solution.py:146
  67.1 0.1 bitcast_dynamic-update-slice_fusion.6
  67.1 0.1 slice.146
  67.2 0.1 slice.148
  67.3 0.1 collective-permute-start.15
  67.4 8.6 %collective-permute-done.17 = bf16[256,768]{1,0:T(8,128)(2,1)S(1)} collective-permute-done((bf16[256,768]{1,0:T(8,128)(2,1)S(1)}, bf16[256,768]{1,0:T(8,128)(2,1)S(1)}, u32[]{:S(2)}, u32[]{:S(2)}) %collective-permute-start.17) | collective-permute-done | bytes 393248 | tf_op jit(solution)/shard_map/ppermute | solution.py:146
  75.9 0.9 collective-permute-start.18
  76.8 7.5 %collective-permute-done.12 = bf16[256,768]{1,0:T(8,128)(2,1)S(1)} collective-permute-done((bf16[256,768]{1,0:T(8,128)(2,1)S(1)}, bf16[256,768]{1,0:T(8,128)(2,1)S(1)}, u32[]{:S(2)}, u32[]{:S(2)}) %collective-permute-start.12) | collective-permute-done | bytes 393248 | tf_op jit(solution)/shard_map/ppermute | solution.py:146
  84.4 0.8 convolution_convert_fusion
  85.2 0.1 collective-permute-start.13
  85.3 1.0 collective-permute-start.14
  86.3 4.3 %collective-permute-done.18 = bf16[256,768]{1,0:T(8,128)(2,1)S(1)} collective-permute-done((bf16[256,768]{1,0:T(8,128)(2,1)S(1)}, bf16[256,768]{1,0:T(8,128)(2,1)S(1)}, u32[]{:S(2)}, u32[]{:S(2)}) %collective-permute-start.18) | collective-permute-done | bytes 393248 | tf_op jit(solution)/shard_map/ppermute | solution.py:146
  90.6 1.0 %convolution_convert_fusion.1 = bf16[512,768]{1,0:T(8,128)(2,1)S(1)} fusion(bf16[1024,512]{1,0:T(8,128)(2,1)S(1)} %bitcast.102, bf16[1024,768]{1,0:T(8,128)(2,1)S(1)} %constant_dynamic-update-slice_fusion), kind=kOutput, calls=%fused_computation.8 | convolution fusion | flops 805699584 | bytes 3407872 | tf_op jit(solution)/shard_map/dot_general | solution.py:103
  91.6 0.1 collective-permute-start.19
  91.7 0.8 fusion.18
  92.5 5.4 %collective-permute-done.14 = bf16[256,768]{1,0:T(8,128)(2,1)S(1)} collective-permute-done((bf16[256,768]{1,0:T(8,128)(2,1)S(1)}, bf16[256,768]{1,0:T(8,128)(2,1)S(1)}, u32[]{:S(2)}, u32[]{:S(2)}) %collective-permute-start.14) | collective-permute-done | bytes 393248 | tf_op jit(solution)/shard_map/ppermute | solution.py:146
  97.9 1.0 %fusion.19.part_ref = f32[512,768]{1,0:T(8,128)S(1)} fusion(bf16[1024,512]{1,0:T(8,128)(2,1)S(1)} %bitcast.101, bf16[1024,768]{1,0:T(8,128)(2,1)S(1)} %constant_dynamic-update-slice_fusion), kind=kOutput, calls=%fused_computation.51 | convolution fusion | flops 805306368 | bytes 4194304 | tf_op jit(solution)/shard_map/dot_general | solution.py:103
  98.9 0.4 add_add_fusion.part_ref
  99.4 1.2 %shard_map.60.refs_1_ = f32[512,1536]{1,0:T(8,128)} custom-call(f32[512,768]{1,0:T(8,128)S(1)} %fusion.19.part_ref, bf16[512,768]{1,0:T(8,128)(2,1)S(1)} %collective-permute-done.19.more_ref), custom_call_target="tpu_custom_call" | custom-call | flops 201326592 | bytes 1572864 | tf_op jit(solution)/shard_map/pallas_call | solution.py:85
  100.6 1.4 %shard_map.61 = f32[512,1536]{1,0:T(8,128)} custom-call(f32[512,768]{1,0:T(8,128)S(1)} %add_add_fusion.part_ref, bf16[256,512]{1,0:T(8,128)(2,1)S(1)} %collective-permute-done.15.more_ref, bf16[256,768]{1,0:T(8,128)(2,1)S(1)} %collective-permute-done.16.refs_0_, f32[512,1536]{1,0:T(8,128)} %shard_map.60.refs_1_), custom_call_target="tpu_custom_call", output_to_operand_aliasing={{}: (3, {})} | custom-call | flops 201326592 | bytes 1572864 | tf_op jit(solution)/shard_map/pallas_call | solution.py:85
  (27 shorter events, 0.3 us)
Async XLA Ops:
  3.5 22.6 %collective-permute-start.4 = (bf16[64,1024]{1,0:T(8,128)(2,1)}, bf16[64,1024]{1,0:T(8,128)(2,1)S(1)}, u32[]{:S(2)}, u32[]{:S(2)}) collective-permute-start(bf16[64,1024]{1,0:T(8,128)(2,1)} %get-tuple-element.7), channel_id=1, source_target_pairs={{0,16},{4,20},{16,24},{20,28},{24,8},{28,12},{8,0},{12,4},{1,17},{... | collective-permute-start | bytes 393224 | tf_op jit(solution)/shard_map/ppermute | solution.py:152
  7.6 20.2 %collective-permute-start.5 = (bf16[64,1024]{1,0:T(8,128)(2,1)}, bf16[64,1024]{1,0:T(8,128)(2,1)S(1)}, u32[]{:S(2)}, u32[]{:S(2)}) collective-permute-start(bf16[64,1024]{1,0:T(8,128)(2,1)} %get-tuple-element.8), channel_id=1, source_target_pairs={{0,24},{4,28},{16,8},{20,12},{24,0},{28,4},{8,16},{12,20},{1,25},{... | collective-permute-start | bytes 393224 | tf_op jit(solution)/shard_map/ppermute | solution.py:152
  8.9 28.8 %collective-permute-start.6 = (bf16[64,1024]{1,0:T(8,128)(2,1)}, bf16[64,1024]{1,0:T(8,128)(2,1)}, u32[]{:S(2)}, u32[]{:S(2)}) collective-permute-start(bf16[64,1024]{1,0:T(8,128)(2,1)} %get-tuple-element.9), channel_id=1, source_target_pairs={{0,8},{4,12},{16,0},{20,4},{24,16},{28,20},{8,24},{12,28},{1,9},{5... | collective-permute-start | bytes 393224 | tf_op jit(solution)/shard_map/ppermute | solution.py:152
  9.7 53.0 %collective-permute-start.11 = (bf16[256,1536]{1,0:T(8,128)(2,1)}, bf16[256,1536]{1,0:T(8,128)(2,1)}, u32[]{:S(2)}, u32[]{:S(2)}) collective-permute-start(bf16[256,1536]{1,0:T(8,128)(2,1)} %param.7), channel_id=1, source_target_pairs={{0,16},{4,20},{16,24},{20,28},{24,8},{28,12},{8,0},{12,4},{1,17},{... | collective-permute-start | bytes 2359304 | tf_op jit(solution)/shard_map/ppermute | solution.py:140
  16.7 2.5 %copy-start = (bf16[256,2048]{1,0:T(8,128)(2,1)}, bf16[256,2048]{1,0:T(8,128)(2,1)S(1)}, u32[]{:S(2)}) copy-start(bf16[256,2048]{1,0:T(8,128)(2,1)S(1)} %fusion.4) | copy-start | bytes 3145732
  16.7 2.4 %copy-start.3 = (bf16[256,1536]{1,0:T(8,128)(2,1)S(1)}, bf16[256,1536]{1,0:T(8,128)(2,1)}, u32[]{:S(2)}) copy-start(bf16[256,1536]{1,0:T(8,128)(2,1)} %param.7) | copy-start | bytes 2359300
  17.6 24.5 %collective-permute-start = (bf16[2,64,2048]{2,1,0:T(8,128)(2,1)}, bf16[2,64,2048]{2,1,0:T(8,128)(2,1)}, u32[]{:S(2)}, u32[]{:S(2)}) collective-permute-start(bf16[2,64,2048]{2,1,0:T(8,128)(2,1)} %pad_maximum_fusion), channel_id=1, source_target_pairs={{0,1},{1,0},{2,3},{3,2},{4,5},{5,4},{6,7},{7,6},{8,9},{9,8},{10,11... | collective-permute-start | bytes 1572872 | tf_op jit(solution)/shard_map/ppermute | solution.py:190
  24.9 12.8 %copy-start.4 = (bf16[64,1024]{1,0:T(8,128)(2,1)S(1)}, bf16[64,1024]{1,0:T(8,128)(2,1)}, u32[]{:S(2)}) copy-start(bf16[64,1024]{1,0:T(8,128)(2,1)} %get-tuple-element.6) | copy-start | bytes 393220
  26.1 18.6 %collective-permute-start.2 = (bf16[2,64,2048]{2,1,0:T(8,128)(2,1)S(1)}, bf16[2,64,2048]{2,1,0:T(8,128)(2,1)S(1)}, u32[]{:S(2)}, u32[]{:S(2)}) collective-permute-start(bf16[2,64,2048]{2,1,0:T(8,128)(2,1)S(1)} %pad_maximum_fusion.1), channel_id=1, source_target_pairs={{0,2},{1,3},{2,0},{3,1},{4,6},{5,7},{6,4},{7,5},{8,10},{9,11},{10,... | collective-permute-start | bytes 1572872 | tf_op jit(solution)/shard_map/ppermute | solution.py:190
  38.7 14.9 %collective-permute-start.7 = (bf16[4,64,1024]{2,1,0:T(8,128)(2,1)S(1)}, bf16[4,64,1024]{2,1,0:T(8,128)(2,1)S(1)}, u32[]{:S(2)}, u32[]{:S(2)}) collective-permute-start(bf16[4,64,1024]{2,1,0:T(8,128)(2,1)S(1)} %pad_maximum_fusion.3), channel_id=1, source_target_pairs={{0,1},{1,0},{2,3},{3,2},{4,5},{5,4},{6,7},{7,6},{8,9},{9,8},{10,11... | collective-permute-start | bytes 1572872 | tf_op jit(solution)/shard_map/ppermute | solution.py:157
  40.2 14.9 %collective-permute-start.8 = (bf16[4,64,1024]{2,1,0:T(8,128)(2,1)S(1)}, bf16[4,64,1024]{2,1,0:T(8,128)(2,1)S(1)}, u32[]{:S(2)}, u32[]{:S(2)}) collective-permute-start(bf16[4,64,1024]{2,1,0:T(8,128)(2,1)S(1)} %pad_maximum_fusion.3), channel_id=1, source_target_pairs={{0,2},{1,3},{2,0},{3,1},{4,6},{5,7},{6,4},{7,5},{8,10},{9,11},{10,... | collective-permute-start | bytes 1572872 | tf_op jit(solution)/shard_map/ppermute | solution.py:157
  41.9 1.2 %copy-start.1 = (bf16[256,2048]{1,0:T(8,128)(2,1)S(1)}, bf16[256,2048]{1,0:T(8,128)(2,1)}, u32[]{:S(2)}) copy-start(bf16[256,2048]{1,0:T(8,128)(2,1)} %copy-done) | copy-start | bytes 3145732
  41.9 2.8 %copy-start.2 = (bf16[256,2048]{1,0:T(8,128)(2,1)S(1)}, bf16[256,2048]{1,0:T(8,128)(2,1)}, u32[]{:S(2)}) copy-start(bf16[256,2048]{1,0:T(8,128)(2,1)} %fusion.7) | copy-start | bytes 3145732
  44.1 16.5 %collective-permute-start.1 = (bf16[1,64,2048]{2,1,0:T(8,128)(2,1)S(1)}, bf16[1,64,2048]{2,1,0:T(8,128)(2,1)S(1)}, u32[]{:S(2)}, u32[]{:S(2)}) collective-permute-start(bf16[1,64,2048]{2,1,0:T(8,128)(2,1)S(1)} %fusion.14), channel_id=1, source_target_pairs={{0,2},{1,3},{2,0},{3,1},{4,6},{5,7},{6,4},{7,5},{8,10},{9,11},{10,... | collective-permute-start | bytes 786440 | tf_op jit(solution)/shard_map/ppermute | solution.py:190
  44.8 17.0 %collective-permute-start.3 = (bf16[1,64,2048]{2,1,0:T(8,128)(2,1)S(1)}, bf16[1,64,2048]{2,1,0:T(8,128)(2,1)S(1)}, u32[]{:S(2)}, u32[]{:S(2)}) collective-permute-start(bf16[1,64,2048]{2,1,0:T(8,128)(2,1)S(1)} %fusion.15), channel_id=1, source_target_pairs={{0,1},{1,0},{2,3},{3,2},{4,5},{5,4},{6,7},{7,6},{8,9},{9,8},{10,11... | collective-permute-start | bytes 786440 | tf_op jit(solution)/shard_map/ppermute | solution.py:190
  53.6 13.4 %collective-permute-start.9 = (bf16[2,64,1024]{2,1,0:T(8,128)(2,1)S(1)}, bf16[2,64,1024]{2,1,0:T(8,128)(2,1)S(1)}, u32[]{:S(2)}, u32[]{:S(2)}) collective-permute-start(bf16[2,64,1024]{2,1,0:T(8,128)(2,1)S(1)} %slice.140), channel_id=1, source_target_pairs={{0,2},{1,3},{2,0},{3,1},{4,6},{5,7},{6,4},{7,5},{8,10},{9,11},{10,... | collective-permute-start | bytes 786440 | tf_op jit(solution)/shard_map/ppermute | solution.py:159
  55.2 11.9 %collective-permute-start.10 = (bf16[2,64,1024]{2,1,0:T(8,128)(2,1)S(1)}, bf16[2,64,1024]{2,1,0:T(8,128)(2,1)S(1)}, u32[]{:S(2)}, u32[]{:S(2)}) collective-permute-start(bf16[2,64,1024]{2,1,0:T(8,128)(2,1)S(1)} %slice.143), channel_id=1, source_target_pairs={{0,1},{1,0},{2,3},{3,2},{4,5},{5,4},{6,7},{7,6},{8,9},{9,8},{10,11... | collective-permute-start | bytes 786440 | tf_op jit(solution)/shard_map/ppermute | solution.py:160
  63.9 12.0 %collective-permute-start.17 = (bf16[256,768]{1,0:T(8,128)(2,1)S(1)}, bf16[256,768]{1,0:T(8,128)(2,1)S(1)}, u32[]{:S(2)}, u32[]{:S(2)}) collective-permute-start(bf16[256,768]{1,0:T(8,128)(2,1)S(1)} %get-tuple-element.14), channel_id=1, source_target_pairs={{0,16},{4,20},{16,24},{20,28},{24,8},{28,12},{8,0},{12,4},{1,17},{... | collective-permute-start | bytes 1179656 | tf_op jit(solution)/shard_map/ppermute | solution.py:146
  64.0 20.4 %collective-permute-start.12 = (bf16[256,768]{1,0:T(8,128)(2,1)S(1)}, bf16[256,768]{1,0:T(8,128)(2,1)S(1)}, u32[]{:S(2)}, u32[]{:S(2)}) collective-permute-start(bf16[256,768]{1,0:T(8,128)(2,1)S(1)} %get-tuple-element.17), channel_id=1, source_target_pairs={{0,16},{4,20},{16,24},{20,28},{24,8},{28,12},{8,0},{12,4},{1,17},{... | collective-permute-start | bytes 1179656 | tf_op jit(solution)/shard_map/ppermute | solution.py:146
  67.3 33.3 %collective-permute-start.15 = (bf16[256,512]{1,0:T(8,128)(2,1)S(1)}, bf16[256,512]{1,0:T(8,128)(2,1)S(1)}, u32[]{:S(2)}, u32[]{:S(2)}) collective-permute-start(bf16[256,512]{1,0:T(8,128)(2,1)S(1)} %bitcast.106), channel_id=1, source_target_pairs={{0,4},{4,0},{8,12},{12,8},{16,20},{20,16},{24,28},{28,24},{1,5},{5... | collective-permute-start | bytes 786440 | tf_op jit(solution)/shard_map/ppermute | solution.py:200
  75.9 14.6 %collective-permute-start.18 = (bf16[256,768]{1,0:T(8,128)(2,1)S(1)}, bf16[256,768]{1,0:T(8,128)(2,1)S(1)}, u32[]{:S(2)}, u32[]{:S(2)}) collective-permute-start(bf16[256,768]{1,0:T(8,128)(2,1)S(1)} %collective-permute-done.17), channel_id=1, source_target_pairs={{0,16},{4,20},{16,24},{20,28},{24,8},{28,12},{8,0},{12,4},{1,17},{... | collective-permute-start | bytes 1179656 | tf_op jit(solution)/shard_map/ppermute | solution.py:146
  85.2 13.7 %collective-permute-start.13 = (bf16[512,768]{1,0:T(8,128)(2,1)S(1)}, bf16[512,768]{1,0:T(8,128)(2,1)S(1)}, u32[]{:S(2)}, u32[]{:S(2)}) collective-permute-start(bf16[512,768]{1,0:T(8,128)(2,1)S(1)} %convolution_convert_fusion), channel_id=1, source_target_pairs={{0,4},{4,0},{8,12},{12,8},{16,20},{20,16},{24,28},{28,24},{1,5},{5... | collective-permute-start | bytes 2359304 | tf_op jit(solution)/shard_map/ppermute | solution.py:204
  85.3 12.6 %collective-permute-start.14 = (bf16[256,768]{1,0:T(8,128)(2,1)S(1)}, bf16[256,768]{1,0:T(8,128)(2,1)S(1)}, u32[]{:S(2)}, u32[]{:S(2)}) collective-permute-start(bf16[256,768]{1,0:T(8,128)(2,1)S(1)} %collective-permute-done.12), channel_id=1, source_target_pairs={{0,16},{4,20},{16,24},{20,28},{24,8},{28,12},{8,0},{12,4},{1,17},{... | collective-permute-start | bytes 1179656 | tf_op jit(solution)/shard_map/ppermute | solution.py:146
  91.6 7.7 %collective-permute-start.19 = (bf16[512,768]{1,0:T(8,128)(2,1)S(1)}, bf16[512,768]{1,0:T(8,128)(2,1)S(1)}, u32[]{:S(2)}, u32[]{:S(2)}) collective-permute-start(bf16[512,768]{1,0:T(8,128)(2,1)S(1)} %convolution_convert_fusion.1), channel_id=1, source_target_pairs={{0,4},{4,0},{8,12},{12,8},{16,20},{20,16},{24,28},{28,24},{1,5},{5... | collective-permute-start | bytes 2359304 | tf_op jit(solution)/shard_map/ppermute | solution.py:204
  97.9 2.7 %collective-permute-start.16 = (bf16[256,768]{1,0:T(8,128)(2,1)S(1)}, bf16[256,768]{1,0:T(8,128)(2,1)S(1)}, u32[]{:S(2)}, u32[]{:S(2)}) collective-permute-start(bf16[256,768]{1,0:T(8,128)(2,1)S(1)} %collective-permute-done.14), channel_id=1, source_target_pairs={{0,4},{4,0},{8,12},{12,8},{16,20},{20,16},{24,28},{28,24},{1,5},{5... | collective-permute-start | bytes 1179656 | tf_op jit(solution)/shard_map/ppermute | solution.py:208

commit v4 on v3

--- a/solution.py
+++ b/solution.py
@@ -116,6 +116,7 @@
     tokens = grad_out.shape[0]
     out_rows = width // n_ctx
     core = lax.axis_index("ctx") % 2
+    chip = lax.axis_index("ctx") // 2
     order = ring_order(chips)
 
     swap = [(i, i ^ 1) for i in range(n_ctx)]
@@ -141,9 +142,16 @@
     moving = [moving[:, ends[h] : ends[h + 1]] for h in range(2)]
     for h in range(2):
         every[h] = lax.dynamic_update_slice(every[h], moving[h], (tokens, 0))
+    fresh = [grad_out[:, ends[h] : ends[h + 1]] for h in range(2)]
+    fresh = lax.optimization_barrier(tuple(fresh))
+    inner = (chip > 0) & (chip < chips - 1)
     for step in range(2, chips):
         for h in range(2):
-            moving[h] = lax.ppermute(moving[h], "ctx", shift(1))
+            pairs = shift(1)
+            if chips == 4 and step == 3:
+                moving[h] = jnp.where(inner, moving[h], fresh[h])
+                pairs = [(i, i ^ 2) for i in range(n_ctx)]
+            moving[h] = lax.ppermute(moving[h], "ctx", pairs)
             if step < chips - 1 or h == 0:
                 every[h] = lax.dynamic_update_slice(every[h], moving[h], (step * tokens, 0))
 

time: 102 us -> 99.7 us (0.977)
  waiting for transfers between devices: 47.7 us -> 46.1 us
  starting transfers between devices: 24 us -> 22.5 us
    ppermute x3, starting transfers between devices: 6.2 us -> 2.48 us  [body(): pieces[step] = lax.ppermute(pieces[step], 'ctx', shift(step))]
    ppermute x1, starting transfers between devices: 2.13 us -> 4.12 us  [body(): moving = lax.ppermute(grad_out, 'ctx', shift(1))]
    ppermute x3, waiting for transfers between devices: 10 us -> 8.94 us  [body(): pieces[step] = lax.ppermute(pieces[step], 'ctx', shift(step))]
  transfers between devices with their start and end apart: 20 -> 20, of which waited for: 7 -> 9; matrix products, arithmetic and copies ran while one was open for 22% -> 23% of each run, Pallas kernels for 1% -> 4%
where the time goes in v4:
time: 99.7 us; the launch traced here: 99.4 us
  waiting for transfers between devices  46.1 us (46%)
  starting transfers between devices  22.5 us (23%)
  matrix products  14.5 us (15%)
  other arithmetic  5.7 us (6%)
  Pallas kernels  5.51 us (6%)
  local copies, waits for them, and re-layouts  3.95 us (4%)
  between operations  1.05 us (1%)
    ppermute x4, waiting for transfers between devices, body(): moving[h] = lax.ppermute(moving[h], 'ctx', pairs)  25.3 us
    dot_general x2, matrix products, body(): lax.dot_general(grad_out, lax.slice_in_dim(weight, h * span, (h + 1) * sp...  10.4 us
    ppermute x3, waiting for transfers between devices, body(): pieces[step] = lax.ppermute(pieces[step], 'ctx', shift(step))  8.94 us
    ppermute x2, waiting for transfers between devices, body(): got[j] = lax.ppermute(pieces, 'tp', peers(j))  8.19 us
    ppermute x4, starting transfers between devices, body(): moving[h] = lax.ppermute(moving[h], 'ctx', pairs)  5.27 us
    ppermute x4, starting transfers between devices, body(): sent = lax.ppermute(sent, 'tp', peers(bit))  4.18 us
    ppermute x1, starting transfers between devices, body(): moving = lax.ppermute(grad_out, 'ctx', shift(1))  4.12 us
    dot_general x5, matrix products, tdot(): lax.dot_general(a, b, (((0,), (0,)), ((), ())), preferred_element_type=jn...  4.09 us
  transfers between devices with their start and end apart: 20, of which 9 were waited for; matrix products, arithmetic and copies ran while one was open for 23% of the time, Pallas kernels for 4%

profile of v4, /device:TPU:0, one launch (start us, length us, event | category | flops | bytes accessed | tf_op | source)
XLA Modules:
  0.0 99.4 jit_solution(8461799838687139380)
XLA Ops:
  0.6 4.1 %collective-permute-start.11 = (bf16[256,1536]{1,0:T(8,128)(2,1)}, bf16[256,1536]{1,0:T(8,128)(2,1)}, u32[]{:S(2)}, u32[]{:S(2)}) collective-permute-start(bf16[256,1536]{1,0:T(8,128)(2,1)} %param.7), channel_id=1, source_target_pairs={{0,16},{4,20},{16,24},{20,28},{24,8},{28,12},{8,0},{12,4},{1,17},{... | collective-permute-start | bytes 2359304 | tf_op jit(solution)/shard_map/ppermute | solution.py:141
  4.7 2.9 %shard_map.59 = (bf16[64,1024]{1,0:T(8,128)(2,1)}, bf16[64,1024]{1,0:T(8,128)(2,1)}, bf16[64,1024]{1,0:T(8,128)(2,1)}, bf16[64,1024]{1,0:T(8,128)(2,1)}) custom-call(bf16[64,4096]{1,0:T(8,128)(2,1)} %codes_ref.1, s32[32,64]{1,0:T(8,128)} %bitcast.108), custom_call_target="tpu_custom_call" | custom-call | flops 524288 | bytes 1048576 | tf_op jit(solution)/shard_map/pallas_call | solution.py:43
  7.6 1.6 %collective-permute-start.4 = (bf16[64,1024]{1,0:T(8,128)(2,1)}, bf16[64,1024]{1,0:T(8,128)(2,1)}, u32[]{:S(2)}, u32[]{:S(2)}) collective-permute-start(bf16[64,1024]{1,0:T(8,128)(2,1)} %get-tuple-element.9), channel_id=1, source_target_pairs={{0,16},{4,20},{16,24},{20,28},{24,8},{28,12},{8,0},{12,4},{1,17},{... | collective-permute-start | bytes 393224 | tf_op jit(solution)/shard_map/ppermute | solution.py:160
  9.2 0.9 collective-permute-start.6
  10.1 4.9 %fusion.4 = bf16[256,2048]{1,0:T(8,128)(2,1)S(1)} fusion(bf16[256,1536]{1,0:T(8,128)(2,1)} %param.7, bf16[4096,1536]{1,0:T(8,128)(2,1)} %param.6), kind=kOutput, calls=%fused_computation.4 | convolution fusion | flops 1611137024 | bytes 8126464 | tf_op jit(solution)/shard_map/dot_general | solution.py:188
  15.0 0.0 copy-start.3
  15.0 0.8 pad_maximum_fusion
  15.9 1.5 %collective-permute-start = (bf16[2,64,2048]{2,1,0:T(8,128)(2,1)}, bf16[2,64,2048]{2,1,0:T(8,128)(2,1)}, u32[]{:S(2)}, u32[]{:S(2)}) collective-permute-start(bf16[2,64,2048]{2,1,0:T(8,128)(2,1)} %pad_maximum_fusion), channel_id=1, source_target_pairs={{0,1},{1,0},{2,3},{3,2},{4,5},{5,4},{6,7},{7,6},{8,9},{9,8},{10,11... | collective-permute-start | bytes 1572872 | tf_op jit(solution)/shard_map/ppermute | solution.py:198
  17.4 0.1 fusion.17
  17.5 5.6 %fusion.7 = bf16[256,2048]{1,0:T(8,128)(2,1)} fusion(bf16[256,1536]{1,0:T(8,128)(2,1)S(1)} %copy-done.3, bf16[4096,1536]{1,0:T(8,128)(2,1)} %param.6), kind=kOutput, calls=%fused_computation.5 | convolution fusion | flops 1611137024 | bytes 8126464 | tf_op jit(solution)/shard_map/dot_general | solution.py:188
  23.0 0.1 dynamic_update_slice.64
  23.1 0.1 dynamic_update_slice.56
  23.3 1.1 %dynamic-slice_bitcast_fusion.1 = (bf16[1,64,2048]{2,1,0:T(8,128)(2,1)S(1)}, bf16[1,64,2048]{2,1,0:T(8,128)(2,1)S(1)}) fusion(bf16[256,2048]{1,0:T(8,128)(2,1)} %fusion.7, s32[]{:T(128)S(6)} %select_n.112, s32[]{:T(128)S(6)} %select_n.111), kind=kLoop, calls=%fused_computation.38 | loop fusion | bytes 1048584 | tf_op jit(solution)/shard_map/stack | solution.py:197
  24.4 0.1 pad_maximum_fusion.1
  24.4 1.4 %collective-permute-done.4 = bf16[64,1024]{1,0:T(8,128)(2,1)} collective-permute-done((bf16[64,1024]{1,0:T(8,128)(2,1)}, bf16[64,1024]{1,0:T(8,128)(2,1)}, u32[]{:S(2)}, u32[]{:S(2)}) %collective-permute-start.4) | collective-permute-done | bytes 131104 | tf_op jit(solution)/shard_map/ppermute | solution.py:160
  25.8 1.5 %collective-permute-start.2 = (bf16[2,64,2048]{2,1,0:T(8,128)(2,1)S(1)}, bf16[2,64,2048]{2,1,0:T(8,128)(2,1)S(1)}, u32[]{:S(2)}, u32[]{:S(2)}) collective-permute-start(bf16[2,64,2048]{2,1,0:T(8,128)(2,1)S(1)} %pad_maximum_fusion.1), channel_id=1, source_target_pairs={{0,2},{1,3},{2,0},{3,1},{4,6},{5,7},{6,4},{7,5},{8,10},{9,11},{10,... | collective-permute-start | bytes 1572872 | tf_op jit(solution)/shard_map/ppermute | solution.py:198
  27.4 3.1 %collective-permute-done.5 = bf16[64,1024]{1,0:T(8,128)(2,1)} collective-permute-done((bf16[64,1024]{1,0:T(8,128)(2,1)}, bf16[64,1024]{1,0:T(8,128)(2,1)}, u32[]{:S(2)}, u32[]{:S(2)}) %collective-permute-start.5) | collective-permute-done | bytes 131104 | tf_op jit(solution)/shard_map/ppermute | solution.py:160
  30.5 4.4 %collective-permute-done.6 = bf16[64,1024]{1,0:T(8,128)(2,1)} collective-permute-done((bf16[64,1024]{1,0:T(8,128)(2,1)}, bf16[64,1024]{1,0:T(8,128)(2,1)}, u32[]{:S(2)}, u32[]{:S(2)}) %collective-permute-start.6) | collective-permute-done | bytes 131104 | tf_op jit(solution)/shard_map/ppermute | solution.py:160
  34.9 1.1 %pad_maximum_fusion.3 = bf16[4,64,1024]{2,1,0:T(8,128)(2,1)S(1)} fusion(bf16[1,64,1024]{2,1,0:T(8,128)(2,1)} %bitcast.16, bf16[1,64,1024]{2,1,0:T(8,128)(2,1)} %bitcast.15, bf16[1,64,1024]{2,1,0:T(8,128)(2,1)} %bitcast.14, bf16[1,64,1024]{2,1,0:T(8,128)(2,1)S(1)} %bitcast.107), kind=kLoop, calls=%fused_computation.12 | loop fusion | flops 786432 | bytes 1048576 | tf_op jit(solution)/shard_map/stack | solution.py:161
  36.0 1.6 %collective-permute-start.7 = (bf16[4,64,1024]{2,1,0:T(8,128)(2,1)S(1)}, bf16[4,64,1024]{2,1,0:T(8,128)(2,1)S(1)}, u32[]{:S(2)}, u32[]{:S(2)}) collective-permute-start(bf16[4,64,1024]{2,1,0:T(8,128)(2,1)S(1)} %pad_maximum_fusion.3), channel_id=1, source_target_pairs={{0,1},{1,0},{2,3},{3,2},{4,5},{5,4},{6,7},{7,6},{8,9},{9,8},{10,11... | collective-permute-start | bytes 1572872 | tf_op jit(solution)/shard_map/ppermute | solution.py:165
  37.6 1.5 %collective-permute-start.8 = (bf16[4,64,1024]{2,1,0:T(8,128)(2,1)S(1)}, bf16[4,64,1024]{2,1,0:T(8,128)(2,1)S(1)}, u32[]{:S(2)}, u32[]{:S(2)}) collective-permute-start(bf16[4,64,1024]{2,1,0:T(8,128)(2,1)S(1)} %pad_maximum_fusion.3), channel_id=1, source_target_pairs={{0,2},{1,3},{2,0},{3,1},{4,6},{5,7},{6,4},{7,5},{8,10},{9,11},{10,... | collective-permute-start | bytes 1572872 | tf_op jit(solution)/shard_map/ppermute | solution.py:165
  39.1 0.1 broadcast.9.clone
  39.2 0.0 copy-start.2
  39.2 0.1 bitcast_dynamic-update-slice_fusion.2
  39.3 0.1 broadcast.9.clone.1
  39.4 0.1 bitcast_dynamic-update-slice_fusion.5
  39.5 0.9 copy-done.1
  40.4 1.0 %fusion.14 = bf16[1,64,2048]{2,1,0:T(8,128)(2,1)S(1)} fusion(bf16[2,64,2048]{2,1,0:T(8,128)(2,1)} %collective-permute-done, bf16[256,2048]{1,0:T(8,128)(2,1)S(1)} %copy-done.1, s32[]{:T(128)S(6)} %select_n.112), kind=kLoop, calls=%fused_computation.25 | loop fusion | flops 524288 | bytes 786436 | tf_op jit(solution)/shard_map/stack | solution.py:197
  41.4 0.6 collective-permute-start.1
  42.0 0.1 fusion.15
  42.1 0.6 collective-permute-start.3
  42.7 8.2 %collective-permute-done.7 = bf16[4,64,1024]{2,1,0:T(8,128)(2,1)S(1)} collective-permute-done((bf16[4,64,1024]{2,1,0:T(8,128)(2,1)S(1)}, bf16[4,64,1024]{2,1,0:T(8,128)(2,1)S(1)}, u32[]{:S(2)}, u32[]{:S(2)}) %collective-permute-start.7) | collective-permute-done | bytes 524320 | tf_op jit(solution)/shard_map/ppermute | solution.py:165
  50.9 1.6 %collective-permute-start.9 = (bf16[2,64,1024]{2,1,0:T(8,128)(2,1)S(1)}, bf16[2,64,1024]{2,1,0:T(8,128)(2,1)S(1)}, u32[]{:S(2)}, u32[]{:S(2)}) collective-permute-start(bf16[2,64,1024]{2,1,0:T(8,128)(2,1)S(1)} %slice.142), channel_id=1, source_target_pairs={{0,2},{1,3},{2,0},{3,1},{4,6},{5,7},{6,4},{7,5},{8,10},{9,11},{10,... | collective-permute-start | bytes 786440 | tf_op jit(solution)/shard_map/ppermute | solution.py:167
  52.5 1.6 %collective-permute-start.10 = (bf16[2,64,1024]{2,1,0:T(8,128)(2,1)S(1)}, bf16[2,64,1024]{2,1,0:T(8,128)(2,1)S(1)}, u32[]{:S(2)}, u32[]{:S(2)}) collective-permute-start(bf16[2,64,1024]{2,1,0:T(8,128)(2,1)S(1)} %slice.145), channel_id=1, source_target_pairs={{0,1},{1,0},{2,3},{3,2},{4,5},{5,4},{6,7},{7,6},{8,9},{9,8},{10,11... | collective-permute-start | bytes 786440 | tf_op jit(solution)/shard_map/ppermute | solution.py:168
  54.1 0.1 bitcast_dynamic-update-slice_fusion.1
  54.2 0.1 bitcast_dynamic-update-slice_fusion
  54.3 3.7 %collective-permute-done.1 = bf16[1,64,2048]{2,1,0:T(8,128)(2,1)S(1)} collective-permute-done((bf16[1,64,2048]{2,1,0:T(8,128)(2,1)S(1)}, bf16[1,64,2048]{2,1,0:T(8,128)(2,1)S(1)}, u32[]{:S(2)}, u32[]{:S(2)}) %collective-permute-start.1) | collective-permute-done | bytes 262176 | tf_op jit(solution)/shard_map/ppermute | solution.py:198
  58.0 1.1 %fusion.12 = bf16[64,2048]{1,0:T(8,128)(2,1)S(1)} fusion(bf16[2,64,2048]{2,1,0:T(8,128)(2,1)} %collective-permute-done, bf16[1,64,2048]{2,1,0:T(8,128)(2,1)S(1)} %collective-permute-done.1, bf16[256,2048]{1,0:T(8,128)(2,1)S(1)} %copy-done.1, s32[]{:T(128)S(6)} %select_n.109), kind=kLoop, calls=%fused_computation.19 | loop fusion | flops 786432 | bytes 1048580 | tf_op jit(solution)/shard_map/convert_element_type | solution.py:107
  59.0 0.1 fusion.10
  59.2 0.8 pad_maximum_fusion.2
  60.0 1.2 %fusion.16 = (bf16[256,768]{1,0:T(8,128)(2,1)S(1)}, bf16[768,768]{1,0:T(8,128)(2,1)S(1)}, bf16[1024,768]{1,0:T(8,128)(2,1)S(1)}, bf16[256,768]{1,0:T(8,128)(2,1)S(1)}) fusion(bf16[256,1536]{1,0:T(8,128)(2,1)} %collective-permute-done.11, bf16[768,768]{1,0:T(8,128)(2,1)S(1)} %dynamic_update_slice.56, bf16[1024,768]{1,0:T(8,128)(2,1)S(1)} %dynamic_update_slice.64), kind=kLoop, calls=%fused_computation.50 | loop fusion | bytes 2359296 | tf_op jit(solution)/shard_map/slice | solution.py:142
  61.2 1.3 %collective-permute-start.17 = (bf16[256,768]{1,0:T(8,128)(2,1)S(1)}, bf16[256,768]{1,0:T(8,128)(2,1)S(1)}, u32[]{:S(2)}, u32[]{:S(2)}) collective-permute-start(bf16[256,768]{1,0:T(8,128)(2,1)S(1)} %get-tuple-element.18), channel_id=1, source_target_pairs={{0,16},{4,20},{16,24},{20,28},{24,8},{28,12},{8,0},{12,4},{1,17},{... | collective-permute-start | bytes 1179656 | tf_op jit(solution)/shard_map/ppermute | solution.py:154
  62.5 1.8 %collective-permute-start.12 = (bf16[256,768]{1,0:T(8,128)(2,1)S(1)}, bf16[256,768]{1,0:T(8,128)(2,1)S(1)}, u32[]{:S(2)}, u32[]{:S(2)}) collective-permute-start(bf16[256,768]{1,0:T(8,128)(2,1)S(1)} %get-tuple-element.21), channel_id=1, source_target_pairs={{0,16},{4,20},{16,24},{20,28},{24,8},{28,12},{8,0},{12,4},{1,17},{... | collective-permute-start | bytes 1179656 | tf_op jit(solution)/shard_map/ppermute | solution.py:154
  64.4 0.1 bitcast_dynamic-update-slice_fusion.6
  64.4 0.1 slice.148
  64.5 0.1 slice.150
  64.6 0.1 collective-permute-start.15
  64.7 8.6 %collective-permute-done.17 = bf16[256,768]{1,0:T(8,128)(2,1)S(1)} collective-permute-done((bf16[256,768]{1,0:T(8,128)(2,1)S(1)}, bf16[256,768]{1,0:T(8,128)(2,1)S(1)}, u32[]{:S(2)}, u32[]{:S(2)}) %collective-permute-start.17) | collective-permute-done | bytes 393248 | tf_op jit(solution)/shard_map/ppermute | solution.py:154
  73.2 0.1 broadcast_select_fusion
  73.3 1.1 %collective-permute-start.18 = (bf16[256,768]{1,0:T(8,128)(2,1)S(1)}, bf16[256,768]{1,0:T(8,128)(2,1)S(1)}, u32[]{:S(2)}, u32[]{:S(2)}) collective-permute-start(bf16[256,768]{1,0:T(8,128)(2,1)S(1)} %get-tuple-element.28), channel_id=1, source_target_pairs={{0,8},{4,12},{8,0},{12,4},{16,24},{20,28},{24,16},{28,20},{1,9},{5... | collective-permute-start | bytes 1179656 | tf_op jit(solution)/shard_map/ppermute | solution.py:154
  74.4 7.2 %collective-permute-done.12 = bf16[256,768]{1,0:T(8,128)(2,1)S(1)} collective-permute-done((bf16[256,768]{1,0:T(8,128)(2,1)S(1)}, bf16[256,768]{1,0:T(8,128)(2,1)S(1)}, u32[]{:S(2)}, u32[]{:S(2)}) %collective-permute-start.12) | collective-permute-done | bytes 393248 | tf_op jit(solution)/shard_map/ppermute | solution.py:154
  81.7 0.1 constant_dynamic-update-slice_fusion.3
  81.8 0.8 convolution_convert_fusion
  82.6 0.1 collective-permute-start.13
  82.7 1.1 %collective-permute-start.14 = (bf16[256,768]{1,0:T(8,128)(2,1)S(1)}, bf16[256,768]{1,0:T(8,128)(2,1)S(1)}, u32[]{:S(2)}, u32[]{:S(2)}) collective-permute-start(bf16[256,768]{1,0:T(8,128)(2,1)S(1)} %get-tuple-element.31), channel_id=1, source_target_pairs={{0,8},{4,12},{8,0},{12,4},{16,24},{20,28},{24,16},{28,20},{1,9},{5... | collective-permute-start | bytes 1179656 | tf_op jit(solution)/shard_map/ppermute | solution.py:154
  83.8 4.1 %collective-permute-done.18 = bf16[256,768]{1,0:T(8,128)(2,1)S(1)} collective-permute-done((bf16[256,768]{1,0:T(8,128)(2,1)S(1)}, bf16[256,768]{1,0:T(8,128)(2,1)S(1)}, u32[]{:S(2)}, u32[]{:S(2)}) %collective-permute-start.18) | collective-permute-done | bytes 393248 | tf_op jit(solution)/shard_map/ppermute | solution.py:154
  87.8 1.0 %convolution_convert_fusion.1 = bf16[512,768]{1,0:T(8,128)(2,1)S(1)} fusion(bf16[1024,512]{1,0:T(8,128)(2,1)S(1)} %bitcast.102, bf16[1024,768]{1,0:T(8,128)(2,1)S(1)} %constant_dynamic-update-slice_fusion), kind=kOutput, calls=%fused_computation.8 | convolution fusion | flops 805699584 | bytes 3407872 | tf_op jit(solution)/shard_map/dot_general | solution.py:103
  88.9 0.1 collective-permute-start.19
  89.0 0.8 fusion.18
  89.8 5.4 %collective-permute-done.14 = bf16[256,768]{1,0:T(8,128)(2,1)S(1)} collective-permute-done((bf16[256,768]{1,0:T(8,128)(2,1)S(1)}, bf16[256,768]{1,0:T(8,128)(2,1)S(1)}, u32[]{:S(2)}, u32[]{:S(2)}) %collective-permute-start.14) | collective-permute-done | bytes 393248 | tf_op jit(solution)/shard_map/ppermute | solution.py:154
  95.2 1.0 %fusion.19.part_ref = f32[512,768]{1,0:T(8,128)S(1)} fusion(bf16[1024,512]{1,0:T(8,128)(2,1)S(1)} %bitcast.101, bf16[1024,768]{1,0:T(8,128)(2,1)S(1)} %constant_dynamic-update-slice_fusion), kind=kOutput, calls=%fused_computation.53 | convolution fusion | flops 805306368 | bytes 4194304 | tf_op jit(solution)/shard_map/dot_general | solution.py:103
  96.3 0.4 add_add_fusion.part_ref
  96.7 1.2 %shard_map.60.refs_1_ = f32[512,1536]{1,0:T(8,128)} custom-call(f32[512,768]{1,0:T(8,128)S(1)} %fusion.19.part_ref, bf16[512,768]{1,0:T(8,128)(2,1)S(1)} %collective-permute-done.19.more_ref), custom_call_target="tpu_custom_call" | custom-call | flops 201326592 | bytes 1572864 | tf_op jit(solution)/shard_map/pallas_call | solution.py:85
  97.9 1.4 %shard_map.61 = f32[512,1536]{1,0:T(8,128)} custom-call(f32[512,768]{1,0:T(8,128)S(1)} %add_add_fusion.part_ref, bf16[256,512]{1,0:T(8,128)(2,1)S(1)} %collective-permute-done.15.more_ref, bf16[256,768]{1,0:T(8,128)(2,1)S(1)} %collective-permute-done.16.refs_0_, f32[512,1536]{1,0:T(8,128)} %shard_map.60.refs_1_), custom_call_target="tpu_custom_call", output_to_operand_aliasing={{}: (3, {})} | custom-call | flops 201326592 | bytes 1572864 | tf_op jit(solution)/shard_map/pallas_call | solution.py:85
  (27 shorter events, 0.2 us)
Async XLA Ops:
  0.6 59.4 %collective-permute-start.11 = (bf16[256,1536]{1,0:T(8,128)(2,1)}, bf16[256,1536]{1,0:T(8,128)(2,1)}, u32[]{:S(2)}, u32[]{:S(2)}) collective-permute-start(bf16[256,1536]{1,0:T(8,128)(2,1)} %param.7), channel_id=1, source_target_pairs={{0,16},{4,20},{16,24},{20,28},{24,8},{28,12},{8,0},{12,4},{1,17},{... | collective-permute-start | bytes 2359304 | tf_op jit(solution)/shard_map/ppermute | solution.py:141
  7.6 18.2 %collective-permute-start.4 = (bf16[64,1024]{1,0:T(8,128)(2,1)}, bf16[64,1024]{1,0:T(8,128)(2,1)}, u32[]{:S(2)}, u32[]{:S(2)}) collective-permute-start(bf16[64,1024]{1,0:T(8,128)(2,1)} %get-tuple-element.9), channel_id=1, source_target_pairs={{0,16},{4,20},{16,24},{20,28},{24,8},{28,12},{8,0},{12,4},{1,17},{... | collective-permute-start | bytes 393224 | tf_op jit(solution)/shard_map/ppermute | solution.py:160
  9.2 21.3 %collective-permute-start.5 = (bf16[64,1024]{1,0:T(8,128)(2,1)}, bf16[64,1024]{1,0:T(8,128)(2,1)}, u32[]{:S(2)}, u32[]{:S(2)}) collective-permute-start(bf16[64,1024]{1,0:T(8,128)(2,1)} %get-tuple-element.10), channel_id=1, source_target_pairs={{0,24},{4,28},{16,8},{20,12},{24,0},{28,4},{8,16},{12,20},{1,25},{... | collective-permute-start | bytes 393224 | tf_op jit(solution)/shard_map/ppermute | solution.py:160
  9.2 25.7 %collective-permute-start.6 = (bf16[64,1024]{1,0:T(8,128)(2,1)}, bf16[64,1024]{1,0:T(8,128)(2,1)}, u32[]{:S(2)}, u32[]{:S(2)}) collective-permute-start(bf16[64,1024]{1,0:T(8,128)(2,1)} %get-tuple-element.11), channel_id=1, source_target_pairs={{0,8},{4,12},{16,0},{20,4},{24,16},{28,20},{8,24},{12,28},{1,9},{5... | collective-permute-start | bytes 393224 | tf_op jit(solution)/shard_map/ppermute | solution.py:160
  14.9 2.4 %copy-start = (bf16[256,2048]{1,0:T(8,128)(2,1)}, bf16[256,2048]{1,0:T(8,128)(2,1)S(1)}, u32[]{:S(2)}) copy-start(bf16[256,2048]{1,0:T(8,128)(2,1)S(1)} %fusion.4) | copy-start | bytes 3145732
  15.0 2.4 %copy-start.3 = (bf16[256,1536]{1,0:T(8,128)(2,1)S(1)}, bf16[256,1536]{1,0:T(8,128)(2,1)}, u32[]{:S(2)}) copy-start(bf16[256,1536]{1,0:T(8,128)(2,1)} %param.7) | copy-start | bytes 2359300
  15.9 23.6 %collective-permute-start = (bf16[2,64,2048]{2,1,0:T(8,128)(2,1)}, bf16[2,64,2048]{2,1,0:T(8,128)(2,1)}, u32[]{:S(2)}, u32[]{:S(2)}) collective-permute-start(bf16[2,64,2048]{2,1,0:T(8,128)(2,1)} %pad_maximum_fusion), channel_id=1, source_target_pairs={{0,1},{1,0},{2,3},{3,2},{4,5},{5,4},{6,7},{7,6},{8,9},{9,8},{10,11... | collective-permute-start | bytes 1572872 | tf_op jit(solution)/shard_map/ppermute | solution.py:198
  23.3 11.6 %copy-start.4 = (bf16[64,1024]{1,0:T(8,128)(2,1)S(1)}, bf16[64,1024]{1,0:T(8,128)(2,1)}, u32[]{:S(2)}) copy-start(bf16[64,1024]{1,0:T(8,128)(2,1)} %get-tuple-element.8) | copy-start | bytes 393220
  25.8 16.2 %collective-permute-start.2 = (bf16[2,64,2048]{2,1,0:T(8,128)(2,1)S(1)}, bf16[2,64,2048]{2,1,0:T(8,128)(2,1)S(1)}, u32[]{:S(2)}, u32[]{:S(2)}) collective-permute-start(bf16[2,64,2048]{2,1,0:T(8,128)(2,1)S(1)} %pad_maximum_fusion.1), channel_id=1, source_target_pairs={{0,2},{1,3},{2,0},{3,1},{4,6},{5,7},{6,4},{7,5},{8,10},{9,11},{10,... | collective-permute-start | bytes 1572872 | tf_op jit(solution)/shard_map/ppermute | solution.py:198
  36.0 14.9 %collective-permute-start.7 = (bf16[4,64,1024]{2,1,0:T(8,128)(2,1)S(1)}, bf16[4,64,1024]{2,1,0:T(8,128)(2,1)S(1)}, u32[]{:S(2)}, u32[]{:S(2)}) collective-permute-start(bf16[4,64,1024]{2,1,0:T(8,128)(2,1)S(1)} %pad_maximum_fusion.3), channel_id=1, source_target_pairs={{0,1},{1,0},{2,3},{3,2},{4,5},{5,4},{6,7},{7,6},{8,9},{9,8},{10,11... | collective-permute-start | bytes 1572872 | tf_op jit(solution)/shard_map/ppermute | solution.py:165
  37.6 14.9 %collective-permute-start.8 = (bf16[4,64,1024]{2,1,0:T(8,128)(2,1)S(1)}, bf16[4,64,1024]{2,1,0:T(8,128)(2,1)S(1)}, u32[]{:S(2)}, u32[]{:S(2)}) collective-permute-start(bf16[4,64,1024]{2,1,0:T(8,128)(2,1)S(1)} %pad_maximum_fusion.3), channel_id=1, source_target_pairs={{0,2},{1,3},{2,0},{3,1},{4,6},{5,7},{6,4},{7,5},{8,10},{9,11},{10,... | collective-permute-start | bytes 1572872 | tf_op jit(solution)/shard_map/ppermute | solution.py:165
  39.2 1.2 %copy-start.1 = (bf16[256,2048]{1,0:T(8,128)(2,1)S(1)}, bf16[256,2048]{1,0:T(8,128)(2,1)}, u32[]{:S(2)}) copy-start(bf16[256,2048]{1,0:T(8,128)(2,1)} %copy-done) | copy-start | bytes 3145732
  39.2 2.8 %copy-start.2 = (bf16[256,2048]{1,0:T(8,128)(2,1)S(1)}, bf16[256,2048]{1,0:T(8,128)(2,1)}, u32[]{:S(2)}) copy-start(bf16[256,2048]{1,0:T(8,128)(2,1)} %fusion.7) | copy-start | bytes 3145732
  41.4 16.5 %collective-permute-start.1 = (bf16[1,64,2048]{2,1,0:T(8,128)(2,1)S(1)}, bf16[1,64,2048]{2,1,0:T(8,128)(2,1)S(1)}, u32[]{:S(2)}, u32[]{:S(2)}) collective-permute-start(bf16[1,64,2048]{2,1,0:T(8,128)(2,1)S(1)} %fusion.14), channel_id=1, source_target_pairs={{0,2},{1,3},{2,0},{3,1},{4,6},{5,7},{6,4},{7,5},{8,10},{9,11},{10,... | collective-permute-start | bytes 786440 | tf_op jit(solution)/shard_map/ppermute | solution.py:198
  42.1 17.0 %collective-permute-start.3 = (bf16[1,64,2048]{2,1,0:T(8,128)(2,1)S(1)}, bf16[1,64,2048]{2,1,0:T(8,128)(2,1)S(1)}, u32[]{:S(2)}, u32[]{:S(2)}) collective-permute-start(bf16[1,64,2048]{2,1,0:T(8,128)(2,1)S(1)} %fusion.15), channel_id=1, source_target_pairs={{0,1},{1,0},{2,3},{3,2},{4,5},{5,4},{6,7},{7,6},{8,9},{9,8},{10,11... | collective-permute-start | bytes 786440 | tf_op jit(solution)/shard_map/ppermute | solution.py:198
  50.9 13.4 %collective-permute-start.9 = (bf16[2,64,1024]{2,1,0:T(8,128)(2,1)S(1)}, bf16[2,64,1024]{2,1,0:T(8,128)(2,1)S(1)}, u32[]{:S(2)}, u32[]{:S(2)}) collective-permute-start(bf16[2,64,1024]{2,1,0:T(8,128)(2,1)S(1)} %slice.142), channel_id=1, source_target_pairs={{0,2},{1,3},{2,0},{3,1},{4,6},{5,7},{6,4},{7,5},{8,10},{9,11},{10,... | collective-permute-start | bytes 786440 | tf_op jit(solution)/shard_map/ppermute | solution.py:167
  52.5 11.9 %collective-permute-start.10 = (bf16[2,64,1024]{2,1,0:T(8,128)(2,1)S(1)}, bf16[2,64,1024]{2,1,0:T(8,128)(2,1)S(1)}, u32[]{:S(2)}, u32[]{:S(2)}) collective-permute-start(bf16[2,64,1024]{2,1,0:T(8,128)(2,1)S(1)} %slice.145), channel_id=1, source_target_pairs={{0,1},{1,0},{2,3},{3,2},{4,5},{5,4},{6,7},{7,6},{8,9},{9,8},{10,11... | collective-permute-start | bytes 786440 | tf_op jit(solution)/shard_map/ppermute | solution.py:168
  61.2 12.0 %collective-permute-start.17 = (bf16[256,768]{1,0:T(8,128)(2,1)S(1)}, bf16[256,768]{1,0:T(8,128)(2,1)S(1)}, u32[]{:S(2)}, u32[]{:S(2)}) collective-permute-start(bf16[256,768]{1,0:T(8,128)(2,1)S(1)} %get-tuple-element.18), channel_id=1, source_target_pairs={{0,16},{4,20},{16,24},{20,28},{24,8},{28,12},{8,0},{12,4},{1,17},{... | collective-permute-start | bytes 1179656 | tf_op jit(solution)/shard_map/ppermute | solution.py:154
  62.5 19.2 %collective-permute-start.12 = (bf16[256,768]{1,0:T(8,128)(2,1)S(1)}, bf16[256,768]{1,0:T(8,128)(2,1)S(1)}, u32[]{:S(2)}, u32[]{:S(2)}) collective-permute-start(bf16[256,768]{1,0:T(8,128)(2,1)S(1)} %get-tuple-element.21), channel_id=1, source_target_pairs={{0,16},{4,20},{16,24},{20,28},{24,8},{28,12},{8,0},{12,4},{1,17},{... | collective-permute-start | bytes 1179656 | tf_op jit(solution)/shard_map/ppermute | solution.py:154
  64.6 33.3 %collective-permute-start.15 = (bf16[256,512]{1,0:T(8,128)(2,1)S(1)}, bf16[256,512]{1,0:T(8,128)(2,1)S(1)}, u32[]{:S(2)}, u32[]{:S(2)}) collective-permute-start(bf16[256,512]{1,0:T(8,128)(2,1)S(1)} %bitcast.106), channel_id=1, source_target_pairs={{0,4},{4,0},{8,12},{12,8},{16,20},{20,16},{24,28},{28,24},{1,5},{5... | collective-permute-start | bytes 786440 | tf_op jit(solution)/shard_map/ppermute | solution.py:208
  73.3 14.5 %collective-permute-start.18 = (bf16[256,768]{1,0:T(8,128)(2,1)S(1)}, bf16[256,768]{1,0:T(8,128)(2,1)S(1)}, u32[]{:S(2)}, u32[]{:S(2)}) collective-permute-start(bf16[256,768]{1,0:T(8,128)(2,1)S(1)} %get-tuple-element.28), channel_id=1, source_target_pairs={{0,8},{4,12},{8,0},{12,4},{16,24},{20,28},{24,16},{28,20},{1,9},{5... | collective-permute-start | bytes 1179656 | tf_op jit(solution)/shard_map/ppermute | solution.py:154
  82.6 13.7 %collective-permute-start.13 = (bf16[512,768]{1,0:T(8,128)(2,1)S(1)}, bf16[512,768]{1,0:T(8,128)(2,1)S(1)}, u32[]{:S(2)}, u32[]{:S(2)}) collective-permute-start(bf16[512,768]{1,0:T(8,128)(2,1)S(1)} %convolution_convert_fusion), channel_id=1, source_target_pairs={{0,4},{4,0},{8,12},{12,8},{16,20},{20,16},{24,28},{28,24},{1,5},{5... | collective-permute-start | bytes 2359304 | tf_op jit(solution)/shard_map/ppermute | solution.py:212
  82.7 12.5 %collective-permute-start.14 = (bf16[256,768]{1,0:T(8,128)(2,1)S(1)}, bf16[256,768]{1,0:T(8,128)(2,1)S(1)}, u32[]{:S(2)}, u32[]{:S(2)}) collective-permute-start(bf16[256,768]{1,0:T(8,128)(2,1)S(1)} %get-tuple-element.31), channel_id=1, source_target_pairs={{0,8},{4,12},{8,0},{12,4},{16,24},{20,28},{24,16},{28,20},{1,9},{5... | collective-permute-start | bytes 1179656 | tf_op jit(solution)/shard_map/ppermute | solution.py:154
  88.9 7.8 %collective-permute-start.19 = (bf16[512,768]{1,0:T(8,128)(2,1)S(1)}, bf16[512,768]{1,0:T(8,128)(2,1)S(1)}, u32[]{:S(2)}, u32[]{:S(2)}) collective-permute-start(bf16[512,768]{1,0:T(8,128)(2,1)S(1)} %convolution_convert_fusion.1), channel_id=1, source_target_pairs={{0,4},{4,0},{8,12},{12,8},{16,20},{20,16},{24,28},{28,24},{1,5},{5... | collective-permute-start | bytes 2359304 | tf_op jit(solution)/shard_map/ppermute | solution.py:212
  95.2 2.7 %collective-permute-start.16 = (bf16[256,768]{1,0:T(8,128)(2,1)S(1)}, bf16[256,768]{1,0:T(8,128)(2,1)S(1)}, u32[]{:S(2)}, u32[]{:S(2)}) collective-permute-start(bf16[256,768]{1,0:T(8,128)(2,1)S(1)} %collective-permute-done.14), channel_id=1, source_target_pairs={{0,4},{4,0},{8,12},{12,8},{16,20},{20,16},{24,28},{28,24},{1,5},{5... | collective-permute-start | bytes 1179656 | tf_op jit(solution)/shard_map/ppermute | solution.py:216
